TPU v7x, 768 devices: a whole 4x8x12 slice. The times are simulated.
768 devices in a mesh: section: 12 (over z_lo, core), tensor: 8 (over y), dp: 8 (over x, z_hi).
Axes of the slice: x: 4, y: 8, z: 12 (z_hi: 2, z_lo: 6; z = z_hi * 6 + z_lo), core: 2. Of those that a mesh axis runs over, the one named last changes fastest.
Arguments:
- residuals: bfloat16 [12, 8, 2, 128, 8192], P('section', 'dp', None, 'tensor'), may hold values from -6 to 6
- norm_gain: bfloat16 [12, 8192], P('section'), may hold values from 0.5 to 1.5
- projection: bfloat16 [12, 8192, 8, 2, 128], P('section', None, 'tensor'), may hold values from -0.0625 to 0.0625
- queries: bfloat16 [12, 8, 2, 128, 8, 1024], P('section', 'dp', None, None, 'tensor'), may hold values from -48 to 48
- output_grad: bfloat16 [12, 8, 2, 128, 8, 1024], P('section', 'dp', None, None, 'tensor'), may hold values from -6 to 6
- section_cotangent: bfloat16 [12, 8, 128, 8192], P('section', 'dp', 'tensor'), may hold values from -6 to 6
- loss_cotangent: bfloat16 [8, 128, 8192], P('dp', 'tensor'), may hold values from -6 to 6
- lengths: int32 [12, 8, 2], P('section', 'dp'), may hold values from 64 to 128
- segments: int32 [12, 8, 2, 128], P('section', 'dp'), may hold values from 0 to 2, never falling along the last dimension, each value on 1 to 64 neighbouring positions
Outputs:
- query_grad: bfloat16 [12, 8, 2, 128, 8, 1024], P('section', 'dp', None, None, 'tensor')
- residual_grad: bfloat16 [12, 8, 128, 8192], P('section', 'dp', 'tensor')
- projection_grad: bfloat16 [12, 8192, 8, 2, 128], P('section', 'dp', 'tensor')
All inputs are finite; a program needn't handle non-finite values.
Results may differ from a plain program's by a relative error of at most 0.015.
Values may be sent and summed in bfloat16 or wider, within the bound.
No kernel may reach another device: no remote copies, remote signals or barrier semaphores. Data moves between devices by JAX's collectives and lax.ppermute only.
A program may use at most 64 MiB of HBM per device.

v0:
```python
import functools

import jax
import jax.numpy as jnp
from jax import lax
from jax.experimental import pallas as pl
from jax.experimental.pallas import tpu as pltpu
from jax.sharding import Mesh
from jax.sharding import PartitionSpec as P

DP = ("dp_0", "dp_1")
EPSILON = 1e-05
MASKED = -1e30
LIFT = 256.0
FARTHEST = 3


def wide(value):
    return value.astype(jnp.float32)


def low(value):
    return value.astype(jnp.bfloat16)


def normalize(residual, gain_wide):
    upcast = wide(residual)
    inverse = lax.rsqrt(jnp.mean(upcast * upcast, axis=-1, keepdims=True) + EPSILON)
    return (low(upcast * inverse * gain_wide), inverse)


def dot(a, b, a_dim, b_dim):
    return lax.dot_general(
        a, b, (((a_dim,), (b_dim,)), ((), ())), preferred_element_type=jnp.float32
    )


def attention_body(
    scalars, segments, pairs, queries, grads, query_grad, pair_grad, pair_rolled, *, count, rows
):
    ticks, row_total, width = queries.shape
    head_size = pairs.shape[2]
    group_size = width // head_size
    scaling = head_size ** (-0.5)
    at_row = lax.broadcasted_iota(jnp.int32, (row_total, row_total), 0)
    at_column = lax.broadcasted_iota(jnp.int32, (row_total, row_total), 1)
    live_row = lax.broadcasted_iota(jnp.int32, (row_total, head_size), 0)
    mine = scalars[ticks]
    for tick in range(ticks):

        def plane(which):
            return jnp.concatenate(
                [
                    pairs[which, (owner * ticks + tick) * rows : (owner * ticks + tick + 1) * rows]
                    for owner in range(count)
                ],
                axis=0,
            )

        keys, values = plane(0), plane(1)
        segment = jnp.broadcast_to(wide(segments[tick : tick + 1]), (row_total, row_total))
        visible = (at_column <= at_row) & (segment == segment.T)
        live = low(wide(live_row < scalars[tick]))

        def stacked(ref):
            return jnp.concatenate(
                [ref[tick, :, h * head_size : (h + 1) * head_size] for h in range(group_size)],
                axis=0,
            )

        query = stacked(queries)
        masked = stacked(grads) * jnp.concatenate([live] * group_size, axis=0)
        scores = dot(query, keys, 1, 1) * scaling
        weight_grad = dot(masked, values, 1, 1)
        scores = jnp.where(jnp.concatenate([visible] * group_size, axis=0), scores, MASKED)
        exponent = jnp.exp(scores - jnp.max(scores, axis=-1, keepdims=True))
        attention = exponent / jnp.sum(exponent, axis=-1, keepdims=True)
        attention_low = low(attention)
        correction = jnp.sum(wide(attention_low) * weight_grad, axis=-1, keepdims=True)
        score_grad = low(attention * (weight_grad - correction))
        value_grad = dot(attention_low, masked, 0, 0)
        key_grad = dot(score_grad, query, 0, 0)
        query_term = low(dot(score_grad, keys, 1, 0) * scaling)
        for head in range(group_size):
            query_grad[tick, :, head * head_size : (head + 1) * head_size] = query_term[
                head * row_total : (head + 1) * row_total
            ]
        for which, grad in ((0, low(key_grad * scaling)), (1, low(value_grad))):
            for owner in range(count):
                piece = grad[owner * rows : (owner + 1) * rows]
                start = (owner * ticks + tick) * rows
                pair_grad[which, start : start + rows] = piece
                ahead = lax.rem(owner - mine - FARTHEST + 2 * count, count)
                place = pl.multiple_of((ahead * ticks + tick) * rows, rows)
                pair_rolled[which, pl.ds(place, rows)] = piece


def attention_grads(scalars, segments, pairs, queries, grads, count, rows):
    vmem = pl.BlockSpec(memory_space=pltpu.VMEM)
    return pl.pallas_call(
        functools.partial(attention_body, count=count, rows=rows),
        out_shape=(
            jax.ShapeDtypeStruct(queries.shape, jnp.bfloat16),
            jax.ShapeDtypeStruct(pairs.shape, jnp.bfloat16),
            jax.ShapeDtypeStruct(pairs.shape, jnp.bfloat16),
        ),
        in_specs=[pl.BlockSpec(memory_space=pltpu.SMEM)] + [vmem] * 4,
        out_specs=(vmem,) * 3,
        compiler_params=pltpu.CompilerParams(vmem_limit_bytes=16 << 20),
        name="attention_grads",
    )(scalars, segments, pairs, queries, grads)


def held_body(source, held, semaphore):
    copy = pltpu.make_async_copy(source, held, semaphore)
    copy.start()
    copy.wait()


def held(value):
    return pl.pallas_call(
        held_body,
        out_shape=pltpu.VMEM(value.shape, value.dtype),
        in_specs=[pl.BlockSpec(memory_space=pltpu.HBM)],
        out_specs=pl.BlockSpec(memory_space=pltpu.VMEM),
        scratch_shapes=[pltpu.SemaphoreType.DMA],
        compiler_params=pltpu.CompilerParams(vmem_limit_bytes=2 << 20),
        name="held",
    )(pltpu.with_memory_space_constraint(value, pltpu.HBM))


def ring_shift(value, axis, step):
    count = lax.axis_size(axis)
    return lax.ppermute(value, axis, [(i, (i + step) % count) for i in range(count)])


def replica_parts(term):
    width, columns = term.shape
    parts = term.reshape(4, width // 4, columns)
    arrived = lax.all_to_all(parts, "dp_0", split_axis=0, concat_axis=0, tiled=True)
    return arrived.reshape(4, 2, width // 8, columns)


def replica_swap(arrived):
    mine = lax.axis_index("dp_1")

    def total(half):
        return wide(lax.dynamic_index_in_dim(arrived, half, 1, keepdims=False)).sum(axis=0)

    sent = low(total(1 - mine))
    swapped = lax.ppermute(sent, "dp_1", [(0, 1), (1, 0)])
    return low(total(mine) + wide(swapped))


def layer(
    residuals,
    norm_gain,
    projection,
    queries,
    output_grad,
    section_cotangent,
    loss_cotangent,
    lengths,
    segments,
):
    local_rows = residuals[0, 0]
    ticks, rows, model_width = local_rows.shape
    count = lax.axis_size("tensor")
    weights = held(projection[0, :, 0])
    gain_wide = wide(norm_gain[0])
    normed_local, inverse = normalize(local_rows, gain_wide)
    lifted = (wide(normed_local) * LIFT).astype(jnp.float16)
    gathered = lax.all_gather(
        lifted.reshape(ticks * rows, model_width), "tensor", axis=0, tiled=True
    )
    normed_all = low(wide(gathered) * (1.0 / LIFT))

    pairs = low(jnp.einsum("rd,dkc->krc", normed_all, weights, preferred_element_type=jnp.float32))
    mine = lax.axis_index("tensor")
    scalars = jnp.concatenate([lengths[0, 0], mine[None].astype(jnp.int32)])
    query_grad, pair_grad, pair_rolled = attention_grads(
        scalars,
        segments[0, 0],
        pairs,
        queries[0, 0].reshape(ticks, count * rows, -1),
        output_grad[0, 0].reshape(ticks, count * rows, -1),
        count,
        rows,
    )

    def replica_term(which):
        return low(dot(normed_all, pair_grad[which], 0, 0))

    def terms(first, last):
        block = pair_rolled[:, first * ticks * rows : last * ticks * rows]
        value = low(jnp.einsum("krc,dkc->rd", block, weights, preferred_element_type=jnp.float32))
        return value.reshape(last - first, ticks * rows, model_width)

    def plus(arrived, own):
        return low(wide(arrived) + wide(own))

    arrived_v = replica_parts(replica_term(1))
    far = terms(0, 3)
    up = ring_shift(far[1, :rows], "tensor", 1)
    down = ring_shift(far[1, rows:], "tensor", -1)
    up = ring_shift(jnp.concatenate([plus(up, far[0, :rows]), far[0, rows:]]), "tensor", 1)
    down = ring_shift(jnp.concatenate([far[2, :rows], plus(down, far[2, rows:])]), "tensor", -1)
    arrived_k = replica_parts(replica_term(0))
    near = terms(3, 8)
    up = ring_shift(plus(up, near[4]), "tensor", 1)
    down = ring_shift(plus(down, near[0]), "tensor", -1)
    up = ring_shift(plus(up, near[3]), "tensor", 1)
    down = ring_shift(plus(down, near[1]), "tensor", -1)
    normed_grad = (wide(near[2]) + wide(up) + wide(down)).reshape(ticks, rows, model_width)

    totals = [replica_swap(arrived_v), replica_swap(arrived_k)]
    projection_grad = jnp.stack([totals[1], totals[0]], axis=1)

    upcast = wide(local_rows)
    scaled = normed_grad * gain_wide
    norm_back = inverse * scaled - upcast * inverse * inverse * inverse * jnp.mean(
        scaled * upcast, axis=-1, keepdims=True
    )
    outgoing = low(wide(section_cotangent[0, 0]) + norm_back[0])
    sections = lax.axis_size("section")
    incoming = lax.ppermute(outgoing, "section", [(s, s - 1) for s in range(1, sections)])
    is_last = lax.axis_index("section") == sections - 1
    incoming = jnp.where(is_last, loss_cotangent[0], incoming)
    residual_grad = low(wide(incoming) + norm_back[1])
    query_all = query_grad.reshape(queries.shape)
    return (query_all, residual_grad[None, None], projection_grad[None, :, None])


def solution(mesh):
    split = Mesh(
        mesh.devices.reshape(mesh.shape["section"], mesh.shape["tensor"], 4, 2),
        ("section", "tensor", "dp_0", "dp_1"),
    )
    placed = (
        P("section", DP, None, "tensor", None),
        P("section", None),
        P("section", None, "tensor", None, None),
        P("section", DP, None, None, "tensor", None),
        P("section", DP, None, None, "tensor", None),
        P("section", DP, "tensor", None),
        P(DP, "tensor", None),
        P("section", DP, None),
        P("section", DP, None, None),
    )
    return jax.shard_map(
        layer,
        mesh=split,
        in_specs=placed,
        out_specs=(
            P("section", DP, None, None, "tensor", None),
            P("section", DP, "tensor", None),
            P("section", DP, "tensor", None, None),
        ),
        check_vma=False,
    )
```

profile of v0, /device:TPU:1, one launch (start us, length us, event | category | flops | bytes accessed | tf_op | source)
XLA Modules:
  0.0 180.8 jit_solution(15758462165651586909)
XLA Ops:
  0.7 2.3 %held.1 = bf16[8192,2,128]{2,1,0:T(2,128)(2,1)S(1)} custom-call(bf16[8192,2,128]{2,1,0:T(2,128)(2,1)} %bitcast.115), custom_call_target="tpu_custom_call" | custom-call | tf_op jit(solution)/shard_map/held/pallas_call | solution.py:121
  5.5 43.0 %all-gather.1 = f16[256,8192]{1,0:T(8,128)(2,1)S(1)} all-gather(f16[32,8192]{1,0:T(8,128)(2,1)S(1)} %multiply_convert_fusion.4), channel_id=1, replica_groups=mesh['section'=12,'tensor'=8,'dp_0'=4,'dp_1'=2] {'tensor'}, dimensions={0}, use_global_device_ids=true | all-gather | bytes 4718592 | tf_op jit(solution)/shard_map/all_gather | solution.py:173
  50.6 3.3 %attention_grads.1 = (bf16[2,128,1024]{2,1,0:T(8,128)(2,1)}, bf16[2,256,128]{2,1,0:T(8,128)(2,1)S(1)}, bf16[2,256,128]{2,1,0:T(8,128)(2,1)S(1)}) custom-call(s32[3]{0:T(128)S(1)} %pad_add_fusion.scalars, s32[2,128]{1,0:T(2,128)S(1)} %bitcast.112, bf16[2,256,128]{2,1,0:T(8,128)(2,1)S(1)} %fusion.12.pairs, bf16[2,128,1024]{2,1,0:T(8,128)(2,1)S(1)} %bitcast.110, ...), custom_call_target="tpu_custom_call" | custom-call | tf_op jit(solution)/shard_map/attention_grads/pallas_call | solution.py:100
  55.5 3.2 %collective-permute-start = (bf16[16,8192]{1,0:T(8,128)(2,1)S(1)}, bf16[16,8192]{1,0:T(8,128)(2,1)S(1)}, u32[]{:S(2)}, u32[]{:S(2)}) collective-permute-start(bf16[16,8192]{1,0:T(8,128)(2,1)S(1)} %get-tuple-element.23), channel_id=1, source_target_pairs={{0,8},{8,16},{16,24},{24,32},{32,40},{40,48},{48,56},{56,0},{1,9},... | collective-permute-start | bytes 786440 | tf_op jit(solution)/shard_map/ppermute | solution.py:134
  58.7 3.3 %collective-permute-start.4 = (bf16[16,8192]{1,0:T(8,128)(2,1)S(1)}, bf16[16,8192]{1,0:T(8,128)(2,1)S(1)}, u32[]{:S(2)}, u32[]{:S(2)}) collective-permute-start(bf16[16,8192]{1,0:T(8,128)(2,1)S(1)} %get-tuple-element.24), channel_id=1, source_target_pairs={{0,56},{8,0},{16,8},{24,16},{32,24},{40,32},{48,40},{56,48},{1,57}... | collective-permute-start | bytes 786440 | tf_op jit(solution)/shard_map/ppermute | solution.py:134
  66.8 2.8 %collective-permute-start.1 = (bf16[32,8192]{1,0:T(8,128)(2,1)}, bf16[32,8192]{1,0:T(8,128)(2,1)}, u32[]{:S(2)}, u32[]{:S(2)}) collective-permute-start(bf16[32,8192]{1,0:T(8,128)(2,1)} %pad_maximum_fusion), channel_id=1, source_target_pairs={{0,8},{8,16},{16,24},{24,32},{32,40},{40,48},{48,56},{56,0},{1,9},... | collective-permute-start | bytes 1572872 | tf_op jit(solution)/shard_map/ppermute | solution.py:134
  70.4 3.7 %collective-permute-start.5 = (bf16[32,8192]{1,0:T(8,128)(2,1)}, bf16[32,8192]{1,0:T(8,128)(2,1)}, u32[]{:S(2)}, u32[]{:S(2)}) collective-permute-start(bf16[32,8192]{1,0:T(8,128)(2,1)} %pad_maximum_fusion.1), channel_id=1, source_target_pairs={{0,56},{8,0},{16,8},{24,16},{32,24},{40,32},{48,40},{56,48},{1,57}... | collective-permute-start | bytes 1572872 | tf_op jit(solution)/shard_map/ppermute | solution.py:134
  74.1 2.6 %convolution_convert_fusion = bf16[8192,128]{1,0:T(8,128)(2,1)} fusion(f16[256,8192]{1,0:T(8,128)(2,1)S(1)} %all-gather.1, bf16[2,256,128]{2,1,0:T(8,128)(2,1)S(1)} %get-tuple-element.8), kind=kOutput, calls=%fused_computation.2 | convolution fusion | flops 544210944 | bytes 6356992 | tf_op jit(solution)/shard_map/dot_general | solution.py:33
  76.7 7.0 %all-to-all-start.1 = ((bf16[4,2048,128]{2,1,0:T(8,128)(2,1)}), bf16[4,2048,128]{2,1,0:T(8,128)(2,1)}, u32[]{:S(2)}, u32[]{:S(2)}) async-start(bf16[4,2048,128]{2,1,0:T(8,128)(2,1)} %bitcast.33), calls=%async_computation.1 | async-start | bytes 4194304 | tf_op jit(solution)/shard_map/all_to_all | solution.py:140
  83.7 3.9 %fusion = bf16[160,8192]{1,0:T(8,128)(2,1)S(1)} fusion(bf16[8192,2,128]{2,1,0:T(2,128)(2,1)} %copy-done, bf16[2,256,128]{2,1,0:T(8,128)(2,1)S(1)} %get-tuple-element.7), kind=kOutput, calls=%fused_computation.1 | convolution fusion | flops 672399360 | bytes 6897664 | tf_op jit(solution)/shard_map/krc,dkc->rd/dot_general | solution.py:196
  87.6 2.4 %add_convert_fusion.3 = (bf16[32,8192]{1,0:T(8,128)(2,1)}, bf16[32,8192]{1,0:T(8,128)(2,1)}) fusion(bf16[32,8192]{1,0:T(8,128)(2,1)} %collective-permute-done.1, bf16[160,8192]{1,0:T(8,128)(2,1)S(1)} %fusion, bf16[32,8192]{1,0:T(8,128)(2,1)} %collective-permute-done.5), kind=kLoop, calls=%fused_computation.34 | loop fusion | flops 2097152 | bytes 3145728 | tf_op jit(solution)/shard_map/convert_element_type | solution.py:23
  91.9 4.6 %collective-permute-start.6 = (bf16[32,8192]{1,0:T(8,128)(2,1)}, bf16[32,8192]{1,0:T(8,128)(2,1)}, u32[]{:S(2)}, u32[]{:S(2)}) collective-permute-start(bf16[32,8192]{1,0:T(8,128)(2,1)} %get-tuple-element.20), channel_id=1, source_target_pairs={{0,56},{8,0},{16,8},{24,16},{32,24},{40,32},{48,40},{56,48},{1,57}... | collective-permute-start | bytes 1572872 | tf_op jit(solution)/shard_map/ppermute | solution.py:134
  96.5 2.6 %convolution_convert_fusion.1 = bf16[8192,128]{1,0:T(8,128)(2,1)} fusion(f16[256,8192]{1,0:T(8,128)(2,1)S(1)} %copy-done.7, bf16[2,256,128]{2,1,0:T(8,128)(2,1)S(1)} %get-tuple-element.8), kind=kOutput, calls=%fused_computation.3 | convolution fusion | flops 544210944 | bytes 6356992 | tf_op jit(solution)/shard_map/dot_general | solution.py:33
  99.2 3.6 %all-to-all-done.1 = bf16[4,2048,128]{2,1,0:T(8,128)(2,1)} async-done(((bf16[4,2048,128]{2,1,0:T(8,128)(2,1)}), bf16[4,2048,128]{2,1,0:T(8,128)(2,1)}, u32[]{:S(2)}, u32[]{:S(2)}) %all-to-all-start.1) | async-done | bytes 2097184 | tf_op jit(solution)/shard_map/all_to_all | solution.py:140
  102.8 4.4 %all-to-all-start = ((bf16[4,2048,128]{2,1,0:T(8,128)(2,1)}), bf16[4,2048,128]{2,1,0:T(8,128)(2,1)}, u32[]{:S(2)}, u32[]{:S(2)}) async-start(bf16[4,2048,128]{2,1,0:T(8,128)(2,1)} %bitcast.117), calls=%async_computation | async-start | bytes 4194304 | tf_op jit(solution)/shard_map/all_to_all | solution.py:140
  107.3 2.4 %add_convert_fusion.2 = (bf16[32,8192]{1,0:T(8,128)(2,1)}, bf16[32,8192]{1,0:T(8,128)(2,1)}) fusion(bf16[32,8192]{1,0:T(8,128)(2,1)} %collective-permute-done.2, bf16[160,8192]{1,0:T(8,128)(2,1)S(1)} %fusion, bf16[32,8192]{1,0:T(8,128)(2,1)} %collective-permute-done.6), kind=kLoop, calls=%fused_computation.33 | loop fusion | flops 2097152 | bytes 3145728 | tf_op jit(solution)/shard_map/convert_element_type | solution.py:23
  109.7 3.1 %collective-permute-start.7 = (bf16[32,8192]{1,0:T(8,128)(2,1)}, bf16[32,8192]{1,0:T(8,128)(2,1)}, u32[]{:S(2)}, u32[]{:S(2)}) collective-permute-start(bf16[32,8192]{1,0:T(8,128)(2,1)} %get-tuple-element.18), channel_id=1, source_target_pairs={{0,56},{8,0},{16,8},{24,16},{32,24},{40,32},{48,40},{56,48},{1,57}... | collective-permute-start | bytes 1572872 | tf_op jit(solution)/shard_map/ppermute | solution.py:134
  116.4 19.8 %collective-permute-start.10 = (bf16[1024,128]{1,0:T(8,128)(2,1)S(1)}, bf16[1024,128]{1,0:T(8,128)(2,1)}, u32[]{:S(2)}, u32[]{:S(2)}) collective-permute-start(bf16[1024,128]{1,0:T(8,128)(2,1)S(1)} %dynamic-slice_reduce_fusion), channel_id=1, source_target_pairs={{0,1},{1,0},{2,3},{3,2},{4,5},{5,4},{6,7},{7,6},{8,9},{9,8},{10,11... | collective-permute-start | bytes 786440 | tf_op jit(solution)/shard_map/ppermute | solution.py:151
  138.3 13.5 %collective-permute-start.9 = (bf16[1024,128]{1,0:T(8,128)(2,1)}, bf16[1024,128]{1,0:T(8,128)(2,1)}, u32[]{:S(2)}, u32[]{:S(2)}) collective-permute-start(bf16[1024,128]{1,0:T(8,128)(2,1)} %dynamic-slice_reduce_fusion.1), channel_id=1, source_target_pairs={{0,1},{1,0},{2,3},{3,2},{4,5},{5,4},{6,7},{7,6},{8,9},{9,8},{10,11... | collective-permute-start | bytes 786440 | tf_op jit(solution)/shard_map/ppermute | solution.py:151
  151.9 2.2 %convert_reduce_fusion = f32[1024,128]{1,0:T(8,128)} fusion(bf16[4,2,1024,128]{3,2,1,0:T(8,128)(2,1)} %bitcast.34, s32[]{:T(128)S(6)} %select_n.19), kind=kLoop, calls=%fused_computation.12 | loop fusion | flops 917504 | bytes 1572868 | tf_op jit(solution)/shard_map/reduce_sum | solution.py:148
  154.1 2.2 %convert_reduce_fusion.1 = f32[1024,128]{1,0:T(8,128)} fusion(bf16[4,2,1024,128]{3,2,1,0:T(8,128)(2,1)} %bitcast.30, s32[]{:T(128)S(6)} %select_n.19), kind=kLoop, calls=%fused_computation.13 | loop fusion | flops 917504 | bytes 1572868 | tf_op jit(solution)/shard_map/reduce_sum | solution.py:148
  156.4 2.6 %fusion.24 = (f32[32]{0:T(128)S(1)}, f32[32,8192]{1,0:T(8,128)}) fusion(bf16[1,1,2,16,8192]{4,3,2,1,0:T(8,128)(2,1)S(1)} %copy-done.5, f32[8192]{0:T(1024)S(1)} %bitcast.119, bf16[32,8192]{1,0:T(8,128)(2,1)} %collective-permute-done.7, bf16[32,8192]{1,0:T(8,128)(2,1)} %collective-permute-done.3, bf16[160,8192]{1,0:T(8,128)(2,1)S(1)} %fusion), kind=kLoop, calls=%fused_computation.27 | loop fusion | flops 2359264 | bytes 3178624 | tf_op jit(solution)/shard_map/reduce_sum | solution.py:221
  161.7 6.8 %collective-permute-start.8 = (bf16[16,8192]{1,0:T(8,128)(2,1)S(1)}, bf16[16,8192]{1,0:T(8,128)(2,1)S(1)}, u32[]{:S(2)}, u32[]{:S(2)}) collective-permute-start(bf16[16,8192]{1,0:T(8,128)(2,1)S(1)} %fusion.28), channel_id=1, source_target_pairs={{64,0},{128,64},{192,128},{256,192},{320,256},{384,320},{448,384},... | collective-permute-start | bytes 786440 | tf_op jit(solution)/shard_map/ppermute | solution.py:226
  169.7 7.9 %collective-permute-done.9 = bf16[1024,128]{1,0:T(8,128)(2,1)} collective-permute-done((bf16[1024,128]{1,0:T(8,128)(2,1)}, bf16[1024,128]{1,0:T(8,128)(2,1)}, u32[]{:S(2)}, u32[]{:S(2)}) %collective-permute-start.9) | collective-permute-done | bytes 262176 | tf_op jit(solution)/shard_map/ppermute | solution.py:151
  (60 shorter events, 26.5 us)
Async XLA Ops:
  0.6 4.3 %copy-start.10 = (bf16[1,8192]{1,0:T(2,128)(2,1)S(1)}, bf16[1,8192]{1,0:T(2,128)(2,1)}, u32[]{:S(2)}) copy-start(bf16[1,8192]{1,0:T(2,128)(2,1)} %param.10) | copy-start | bytes 49156
  0.6 4.3 %copy-start.5 = (bf16[1,1,2,16,8192]{4,3,2,1,0:T(8,128)(2,1)S(1)}, bf16[1,1,2,16,8192]{4,3,2,1,0:T(8,128)(2,1)}, u32[]{:S(2)}) copy-start(bf16[1,1,2,16,8192]{4,3,2,1,0:T(8,128)(2,1)} %param.9) | copy-start | bytes 1572868
  2.9 2.0 %copy-start = (bf16[8192,2,128]{2,1,0:T(2,128)(2,1)}, bf16[8192,2,128]{2,1,0:T(2,128)(2,1)S(1)}, u32[]{:S(2)}) copy-start(bf16[8192,2,128]{2,1,0:T(2,128)(2,1)S(1)} %held.1) | copy-start | bytes 12582916
  4.9 43.7 %copy-start.11 = (s32[1,1,2]{2,1,0:T(1,128)S(1)}, s32[1,1,2]{2,1,0:T(1,128)}, u32[]{:S(2)}) copy-start(s32[1,1,2]{2,1,0:T(1,128)} %param.16) | copy-start | bytes 28
  5.2 43.4 %copy-start.1 = (bf16[8192,2,128]{2,1,0:T(2,128)(2,1)S(1)}, bf16[8192,2,128]{2,1,0:T(2,128)(2,1)}, u32[]{:S(2)}) copy-start(bf16[8192,2,128]{2,1,0:T(2,128)(2,1)} %copy-done) | copy-start | bytes 12582916
  48.6 25.6 %copy-start.6 = (f16[256,8192]{1,0:T(8,128)(2,1)}, f16[256,8192]{1,0:T(8,128)(2,1)S(1)}, u32[]{:S(2)}) copy-start(f16[256,8192]{1,0:T(8,128)(2,1)S(1)} %all-gather.1) | copy-start | bytes 12582916
  48.6 2.0 %copy-start.3 = (bf16[1,1,2,128,1,1024]{5,3,4,2,1,0:T(8,128)(2,1)S(1)}, bf16[1,1,2,128,1,1024]{5,3,4,2,1,0:T(8,128)(2,1)}, u32[]{:S(2)}) copy-start(bf16[1,1,2,128,1,1024]{5,3,4,2,1,0:T(8,128)(2,1)} %param.13) | copy-start | bytes 1572868
  48.6 2.0 %copy-start.4 = (s32[1,1,2,128]{3,2,1,0:T(2,128)S(1)}, s32[1,1,2,128]{3,2,1,0:T(2,128)}, u32[]{:S(2)}) copy-start(s32[1,1,2,128]{3,2,1,0:T(2,128)} %param.17) | copy-start | bytes 3076
  55.5 8.3 %collective-permute-start = (bf16[16,8192]{1,0:T(8,128)(2,1)S(1)}, bf16[16,8192]{1,0:T(8,128)(2,1)S(1)}, u32[]{:S(2)}, u32[]{:S(2)}) collective-permute-start(bf16[16,8192]{1,0:T(8,128)(2,1)S(1)} %get-tuple-element.23), channel_id=1, source_target_pairs={{0,8},{8,16},{16,24},{24,32},{32,40},{40,48},{48,56},{56,0},{1,9},... | collective-permute-start | bytes 786440 | tf_op jit(solution)/shard_map/ppermute | solution.py:134
  58.7 7.1 %collective-permute-start.4 = (bf16[16,8192]{1,0:T(8,128)(2,1)S(1)}, bf16[16,8192]{1,0:T(8,128)(2,1)S(1)}, u32[]{:S(2)}, u32[]{:S(2)}) collective-permute-start(bf16[16,8192]{1,0:T(8,128)(2,1)S(1)} %get-tuple-element.24), channel_id=1, source_target_pairs={{0,56},{8,0},{16,8},{24,16},{32,24},{40,32},{48,40},{56,48},{1,57}... | collective-permute-start | bytes 786440 | tf_op jit(solution)/shard_map/ppermute | solution.py:134
  66.8 20.8 %collective-permute-start.1 = (bf16[32,8192]{1,0:T(8,128)(2,1)}, bf16[32,8192]{1,0:T(8,128)(2,1)}, u32[]{:S(2)}, u32[]{:S(2)}) collective-permute-start(bf16[32,8192]{1,0:T(8,128)(2,1)} %pad_maximum_fusion), channel_id=1, source_target_pairs={{0,8},{8,16},{16,24},{24,32},{32,40},{40,48},{48,56},{56,0},{1,9},... | collective-permute-start | bytes 1572872 | tf_op jit(solution)/shard_map/ppermute | solution.py:134
  70.4 17.2 %collective-permute-start.5 = (bf16[32,8192]{1,0:T(8,128)(2,1)}, bf16[32,8192]{1,0:T(8,128)(2,1)}, u32[]{:S(2)}, u32[]{:S(2)}) collective-permute-start(bf16[32,8192]{1,0:T(8,128)(2,1)} %pad_maximum_fusion.1), channel_id=1, source_target_pairs={{0,56},{8,0},{16,8},{24,16},{32,24},{40,32},{48,40},{56,48},{1,57}... | collective-permute-start | bytes 1572872 | tf_op jit(solution)/shard_map/ppermute | solution.py:134
  76.7 26.0 %all-to-all-start.1 = ((bf16[4,2048,128]{2,1,0:T(8,128)(2,1)}), bf16[4,2048,128]{2,1,0:T(8,128)(2,1)}, u32[]{:S(2)}, u32[]{:S(2)}) async-start(bf16[4,2048,128]{2,1,0:T(8,128)(2,1)} %bitcast.33), calls=%async_computation.1 | async-start | bytes 4194304 | tf_op jit(solution)/shard_map/all_to_all | solution.py:140
  83.7 12.8 %copy-start.7 = (f16[256,8192]{1,0:T(8,128)(2,1)S(1)}, f16[256,8192]{1,0:T(8,128)(2,1)}, u32[]{:S(2)}) copy-start(f16[256,8192]{1,0:T(8,128)(2,1)} %copy-done.6) | copy-start | bytes 12582916
  90.0 17.2 %collective-permute-start.2 = (bf16[32,8192]{1,0:T(8,128)(2,1)}, bf16[32,8192]{1,0:T(8,128)(2,1)}, u32[]{:S(2)}, u32[]{:S(2)}) collective-permute-start(bf16[32,8192]{1,0:T(8,128)(2,1)} %get-tuple-element.19), channel_id=1, source_target_pairs={{0,8},{8,16},{16,24},{24,32},{32,40},{40,48},{48,56},{56,0},{1,9},... | collective-permute-start | bytes 1572872 | tf_op jit(solution)/shard_map/ppermute | solution.py:134
  91.9 15.3 %collective-permute-start.6 = (bf16[32,8192]{1,0:T(8,128)(2,1)}, bf16[32,8192]{1,0:T(8,128)(2,1)}, u32[]{:S(2)}, u32[]{:S(2)}) collective-permute-start(bf16[32,8192]{1,0:T(8,128)(2,1)} %get-tuple-element.20), channel_id=1, source_target_pairs={{0,56},{8,0},{16,8},{24,16},{32,24},{40,32},{48,40},{56,48},{1,57}... | collective-permute-start | bytes 1572872 | tf_op jit(solution)/shard_map/ppermute | solution.py:134
  102.8 33.4 %all-to-all-start = ((bf16[4,2048,128]{2,1,0:T(8,128)(2,1)}), bf16[4,2048,128]{2,1,0:T(8,128)(2,1)}, u32[]{:S(2)}, u32[]{:S(2)}) async-start(bf16[4,2048,128]{2,1,0:T(8,128)(2,1)} %bitcast.117), calls=%async_computation | async-start | bytes 4194304 | tf_op jit(solution)/shard_map/all_to_all | solution.py:140
  109.7 46.7 %collective-permute-start.7 = (bf16[32,8192]{1,0:T(8,128)(2,1)}, bf16[32,8192]{1,0:T(8,128)(2,1)}, u32[]{:S(2)}, u32[]{:S(2)}) collective-permute-start(bf16[32,8192]{1,0:T(8,128)(2,1)} %get-tuple-element.18), channel_id=1, source_target_pairs={{0,56},{8,0},{16,8},{24,16},{32,24},{40,32},{48,40},{56,48},{1,57}... | collective-permute-start | bytes 1572872 | tf_op jit(solution)/shard_map/ppermute | solution.py:134
  112.8 43.6 %collective-permute-start.3 = (bf16[32,8192]{1,0:T(8,128)(2,1)}, bf16[32,8192]{1,0:T(8,128)(2,1)}, u32[]{:S(2)}, u32[]{:S(2)}) collective-permute-start(bf16[32,8192]{1,0:T(8,128)(2,1)} %get-tuple-element.17), channel_id=1, source_target_pairs={{0,8},{8,16},{16,24},{24,32},{32,40},{40,48},{48,56},{56,0},{1,9},... | collective-permute-start | bytes 1572872 | tf_op jit(solution)/shard_map/ppermute | solution.py:134
  116.4 52.2 %collective-permute-start.10 = (bf16[1024,128]{1,0:T(8,128)(2,1)S(1)}, bf16[1024,128]{1,0:T(8,128)(2,1)}, u32[]{:S(2)}, u32[]{:S(2)}) collective-permute-start(bf16[1024,128]{1,0:T(8,128)(2,1)S(1)} %dynamic-slice_reduce_fusion), channel_id=1, source_target_pairs={{0,1},{1,0},{2,3},{3,2},{4,5},{5,4},{6,7},{7,6},{8,9},{9,8},{10,11... | collective-permute-start | bytes 786440 | tf_op jit(solution)/shard_map/ppermute | solution.py:151
  138.3 39.3 %collective-permute-start.9 = (bf16[1024,128]{1,0:T(8,128)(2,1)}, bf16[1024,128]{1,0:T(8,128)(2,1)}, u32[]{:S(2)}, u32[]{:S(2)}) collective-permute-start(bf16[1024,128]{1,0:T(8,128)(2,1)} %dynamic-slice_reduce_fusion.1), channel_id=1, source_target_pairs={{0,1},{1,0},{2,3},{3,2},{4,5},{5,4},{6,7},{7,6},{8,9},{9,8},{10,11... | collective-permute-start | bytes 786440 | tf_op jit(solution)/shard_map/ppermute | solution.py:151
  159.0 18.7 %copy-start.8 = (f32[1024,128]{1,0:T(8,128)S(1)}, f32[1024,128]{1,0:T(8,128)}, u32[]{:S(2)}) copy-start(f32[1024,128]{1,0:T(8,128)} %convert_reduce_fusion.1) | copy-start | bytes 1572868
  159.0 21.1 %copy-start.9 = (bf16[1,16,8192]{2,1,0:T(8,128)(2,1)S(1)}, bf16[1,16,8192]{2,1,0:T(8,128)(2,1)}, u32[]{:S(2)}) copy-start(bf16[1,16,8192]{2,1,0:T(8,128)(2,1)} %param.15) | copy-start | bytes 786436
  161.7 18.3 %collective-permute-start.8 = (bf16[16,8192]{1,0:T(8,128)(2,1)S(1)}, bf16[16,8192]{1,0:T(8,128)(2,1)S(1)}, u32[]{:S(2)}, u32[]{:S(2)}) collective-permute-start(bf16[16,8192]{1,0:T(8,128)(2,1)S(1)} %fusion.28), channel_id=1, source_target_pairs={{64,0},{128,64},{192,128},{256,192},{320,256},{384,320},{448,384},... | collective-permute-start | bytes 786440 | tf_op jit(solution)/shard_map/ppermute | solution.py:226
  (1 other events, 1.4 us)
where the time goes:
time: 182 us; the launch traced here: 181 us
  starting transfers between devices  76.3 us (42%)
  blocking collectives  43 us (24%)
  other arithmetic  23.4 us (13%)
  waiting for transfers between devices  15.4 us (8%)
  matrix products  11.8 us (6%)
  Pallas kernels  5.59 us (3%)
  local copies, waits for them, and re-layouts  4.29 us (2%)
    all_gather x1, blocking collectives, layer(): lax.all_gather(lifted.reshape(ticks * rows, model_width), 'tensor', axis=...  43 us
    ppermute x2, starting transfers between devices, replica_swap(): swapped = lax.ppermute(sent, 'dp_1', [(0, 1), (1, 0)])  33.4 us
    ppermute x8, starting transfers between devices, ring_shift(): lax.ppermute(value, axis, [(i, (i + step) % count) for i in range(count)])  24.7 us
    all_to_all x2, starting transfers between devices, replica_parts(): lax.all_to_all(parts, 'dp_0', split_axis=0, concat_axis=0, tiled=True)  11.4 us
    reduce_sum x4, other arithmetic, total(): wide(lax.dynamic_index_in_dim(arrived, half, 1, keepdims=False)).sum(axis=0)  8 us
    ppermute x2, waiting for transfers between devices, replica_swap(): swapped = lax.ppermute(sent, 'dp_1', [(0, 1), (1, 0)])  7.91 us
    ppermute x1, starting transfers between devices, layer(): lax.ppermute(outgoing, 'section', [(s, s - 1) for s in range(1, sections)])  6.85 us
    convert_element_type x4, other arithmetic, low(): return value.astype(jnp.bfloat16)  5.94 us
  transfers between devices with their start and end apart: 13, of which 4 were waited for; matrix products, arithmetic and copies ran while one was open for 17% of the time, Pallas kernels for 0%

commit v1 on v0

--- a/solution.py
+++ b/solution.py
@@ -36,7 +36,7 @@
 
 
 def attention_body(
-    scalars, segments, pairs, queries, grads, query_grad, pair_grad, pair_rolled, *, count, rows
+    lengths, segments, pairs, queries, grads, query_grad, pair_grad, pair_rolled, *, count, rows
 ):
     ticks, row_total, width = queries.shape
     head_size = pairs.shape[2]
@@ -45,7 +45,7 @@
     at_row = lax.broadcasted_iota(jnp.int32, (row_total, row_total), 0)
     at_column = lax.broadcasted_iota(jnp.int32, (row_total, row_total), 1)
     live_row = lax.broadcasted_iota(jnp.int32, (row_total, head_size), 0)
-    mine = scalars[ticks]
+    mine = lax.axis_index("tensor")
     for tick in range(ticks):
 
         def plane(which):
@@ -60,7 +60,7 @@
         keys, values = plane(0), plane(1)
         segment = jnp.broadcast_to(wide(segments[tick : tick + 1]), (row_total, row_total))
         visible = (at_column <= at_row) & (segment == segment.T)
-        live = low(wide(live_row < scalars[tick]))
+        live = low(wide(live_row < lengths[tick]))
 
         def stacked(ref):
             return jnp.concatenate(
@@ -95,7 +95,7 @@
                 pair_rolled[which, pl.ds(place, rows)] = piece
 
 
-def attention_grads(scalars, segments, pairs, queries, grads, count, rows):
+def attention_grads(lengths, segments, pairs, queries, grads, count, rows):
     vmem = pl.BlockSpec(memory_space=pltpu.VMEM)
     return pl.pallas_call(
         functools.partial(attention_body, count=count, rows=rows),
@@ -108,25 +108,7 @@
         out_specs=(vmem,) * 3,
         compiler_params=pltpu.CompilerParams(vmem_limit_bytes=16 << 20),
         name="attention_grads",
-    )(scalars, segments, pairs, queries, grads)
-
-
-def held_body(source, held, semaphore):
-    copy = pltpu.make_async_copy(source, held, semaphore)
-    copy.start()
-    copy.wait()
-
-
-def held(value):
-    return pl.pallas_call(
-        held_body,
-        out_shape=pltpu.VMEM(value.shape, value.dtype),
-        in_specs=[pl.BlockSpec(memory_space=pltpu.HBM)],
-        out_specs=pl.BlockSpec(memory_space=pltpu.VMEM),
-        scratch_shapes=[pltpu.SemaphoreType.DMA],
-        compiler_params=pltpu.CompilerParams(vmem_limit_bytes=2 << 20),
-        name="held",
-    )(pltpu.with_memory_space_constraint(value, pltpu.HBM))
+    )(lengths, segments, pairs, queries, grads)
 
 
 def ring_shift(value, axis, step):
@@ -134,22 +116,30 @@
     return lax.ppermute(value, axis, [(i, (i + step) % count) for i in range(count)])
 
 
-def replica_parts(term):
+def replica_parts(term, own):
     width, columns = term.shape
-    parts = term.reshape(4, width // 4, columns)
-    arrived = lax.all_to_all(parts, "dp_0", split_axis=0, concat_axis=0, tiled=True)
-    return arrived.reshape(4, 2, width // 8, columns)
-
-
-def replica_swap(arrived):
-    mine = lax.axis_index("dp_1")
-
-    def total(half):
-        return wide(lax.dynamic_index_in_dim(arrived, half, 1, keepdims=False)).sum(axis=0)
-
-    sent = low(total(1 - mine))
-    swapped = lax.ppermute(sent, "dp_1", [(0, 1), (1, 0)])
-    return low(total(mine) + wide(swapped))
+    quarter, half = width // 4, width // 8
+
+    def part(at, length):
+        return lax.dynamic_slice(
+            term, (own[at], own[5]), (length, columns), allow_negative_indices=False
+        )
+
+    others = [ring_shift(part(k, quarter), "dp_0", k) for k in (1, 3, 2)]
+    return [part(0, half), part(4, half)] + others
+
+
+def replica_sum(parts, upper):
+    half = parts[0].shape[0]
+    low_half, high_half = (
+        wide(parts[index]) + sum(wide(other[at : at + half]) for other in parts[2:])
+        for index, at in ((0, 0), (1, half))
+    )
+    return low(jnp.where(upper, low_half, high_half)), jnp.where(upper, high_half, low_half)
+
+
+def swapped(value):
+    return wide(lax.ppermute(value, "dp_1", [(0, 1), (1, 0)]))
 
 
 def layer(
@@ -163,23 +153,26 @@
     lengths,
     segments,
 ):
-    local_rows = residuals[0, 0]
-    ticks, rows, model_width = local_rows.shape
+    _, _, ticks, rows, model_width = residuals.shape
+    local_rows = residuals.reshape(ticks * rows, model_width)
     count = lax.axis_size("tensor")
-    weights = held(projection[0, :, 0])
+    sections = lax.axis_size("section")
+    weights = projection[0, :, 0]
     gain_wide = wide(norm_gain[0])
     normed_local, inverse = normalize(local_rows, gain_wide)
     lifted = (wide(normed_local) * LIFT).astype(jnp.float16)
-    gathered = lax.all_gather(
-        lifted.reshape(ticks * rows, model_width), "tensor", axis=0, tiled=True
-    )
+    place = lax.axis_index("dp_0")
+    own = [((place + k) & 3) * (model_width // 4) for k in range(4)]
+    own = own + [own[0] + model_width // 8, jnp.zeros((), jnp.int32)]
+    upper = lax.axis_index("dp_1") == 1
+    is_last = lax.axis_index("section") == sections - 1
+    lifted, own, upper, is_last = lax.optimization_barrier((lifted, own, upper, is_last))
+    gathered = lax.all_gather(lifted, "tensor", axis=0, tiled=True)
     normed_all = low(wide(gathered) * (1.0 / LIFT))
 
     pairs = low(jnp.einsum("rd,dkc->krc", normed_all, weights, preferred_element_type=jnp.float32))
-    mine = lax.axis_index("tensor")
-    scalars = jnp.concatenate([lengths[0, 0], mine[None].astype(jnp.int32)])
     query_grad, pair_grad, pair_rolled = attention_grads(
-        scalars,
+        lengths[0, 0],
         segments[0, 0],
         pairs,
         queries[0, 0].reshape(ticks, count * rows, -1),
@@ -191,42 +184,42 @@
     def replica_term(which):
         return low(dot(normed_all, pair_grad[which], 0, 0))
 
-    def terms(first, last):
-        block = pair_rolled[:, first * ticks * rows : last * ticks * rows]
-        value = low(jnp.einsum("krc,dkc->rd", block, weights, preferred_element_type=jnp.float32))
-        return value.reshape(last - first, ticks * rows, model_width)
-
-    def plus(arrived, own):
-        return low(wide(arrived) + wide(own))
-
-    arrived_v = replica_parts(replica_term(1))
-    far = terms(0, 3)
-    up = ring_shift(far[1, :rows], "tensor", 1)
-    down = ring_shift(far[1, rows:], "tensor", -1)
-    up = ring_shift(jnp.concatenate([plus(up, far[0, :rows]), far[0, rows:]]), "tensor", 1)
-    down = ring_shift(jnp.concatenate([far[2, :rows], plus(down, far[2, rows:])]), "tensor", -1)
-    arrived_k = replica_parts(replica_term(0))
-    near = terms(3, 8)
-    up = ring_shift(plus(up, near[4]), "tensor", 1)
-    down = ring_shift(plus(down, near[0]), "tensor", -1)
-    up = ring_shift(plus(up, near[3]), "tensor", 1)
-    down = ring_shift(plus(down, near[1]), "tensor", -1)
-    normed_grad = (wide(near[2]) + wide(up) + wide(down)).reshape(ticks, rows, model_width)
-
-    totals = [replica_swap(arrived_v), replica_swap(arrived_k)]
-    projection_grad = jnp.stack([totals[1], totals[0]], axis=1)
+    def plus(arrived, mine):
+        return low(wide(arrived) + wide(mine))
+
+    terms = low(
+        jnp.einsum("krc,dkc->rd", pair_rolled, weights, preferred_element_type=jnp.float32)
+    ).reshape(count, ticks * rows, model_width)
+
+    def term(ahead):
+        return terms[(ahead - FARTHEST) % count]
+
+    sent_v, kept_v = replica_sum(replica_parts(replica_term(1), own), upper)
+    parts_k = replica_parts(replica_term(0), own)
+    parts_k, _ = lax.optimization_barrier((parts_k, sent_v))
+    sent_k, kept_k = replica_sum(parts_k, upper)
+    across = ring_shift(term(4), "tensor", 4)
+    up = ring_shift(term(3), "tensor", 1)
+    down = ring_shift(term(-3), "tensor", -1)
+    up = ring_shift(plus(up, term(2)), "tensor", 1)
+    down = ring_shift(plus(down, term(-2)), "tensor", -1)
+    up = ring_shift(plus(up, term(1)), "tensor", 1)
+    down = ring_shift(plus(down, term(-1)), "tensor", -1)
+    normed_grad = wide(term(0)) + wide(up) + wide(down) + wide(across)
+
+    values_total = low(kept_v + swapped(sent_v))
+    keys_total = low(kept_k + swapped(sent_k))
+    projection_grad = jnp.stack([keys_total, values_total], axis=1)
 
     upcast = wide(local_rows)
     scaled = normed_grad * gain_wide
     norm_back = inverse * scaled - upcast * inverse * inverse * inverse * jnp.mean(
         scaled * upcast, axis=-1, keepdims=True
     )
-    outgoing = low(wide(section_cotangent[0, 0]) + norm_back[0])
-    sections = lax.axis_size("section")
+    outgoing = low(wide(section_cotangent[0, 0]) + norm_back[:rows])
     incoming = lax.ppermute(outgoing, "section", [(s, s - 1) for s in range(1, sections)])
-    is_last = lax.axis_index("section") == sections - 1
     incoming = jnp.where(is_last, loss_cotangent[0], incoming)
-    residual_grad = low(wide(incoming) + norm_back[1])
+    residual_grad = low(wide(incoming) + norm_back[rows:])
     query_all = query_grad.reshape(queries.shape)
     return (query_all, residual_grad[None, None], projection_grad[None, :, None])
 

time: 182 us -> 186 us (1.022); the launches traced: 181 us -> 183 us
  waiting for transfers between devices: 15.4 us -> 44.5 us
  other arithmetic: 23.4 us -> 7.27 us
  matrix products: 11.8 us -> 5.19 us
  Pallas kernels: 5.59 us -> 3.32 us
    ppermute x8 -> x13, waiting for transfers between devices: 3.87 us -> 36.2 us  [ring_shift(): lax.ppermute(value, axis, [(i, (i + step) % count) for i in range(count)])]
    ppermute x8 -> x13, starting transfers between devices: 24.7 us -> 47.4 us  [ring_shift(): lax.ppermute(value, axis, [(i, (i + step) % count) for i in range(count)])]
    ppermute x2, starting transfers between devices: 33.4 us -> 20 us  [swapped(): return wide(lax.ppermute(value, 'dp_1', [(0, 1), (1, 0)]))]
    all_to_all x2 -> x0, starting transfers between devices: 11.4 us -> none  [replica_parts(): lax.all_to_all(parts, 'dp_0', split_axis=0, concat_axis=0, tiled=True)]
    reduce_sum x4 -> x0, other arithmetic: 8 us -> none  [total(): wide(lax.dynamic_index_in_dim(arrived, half, 1, keepdims=False)).sum(axis=0)]
    convert_element_type x4 -> x5, other arithmetic: 5.94 us -> 1.21 us  [low(): return value.astype(jnp.bfloat16)]
    dot_general x2 -> x1, matrix products: 5.27 us -> 1.3 us  [layer(): jnp.einsum('krc,dkc->rd', pair_rolled, weights, preferred_element_type=jn...]
    all_to_all x2 -> x0, waiting for transfers between devices: 3.63 us -> none  [replica_parts(): lax.all_to_all(parts, 'dp_0', split_axis=0, concat_axis=0, tiled=True)]
  transfers between devices with their start and end apart: 13 -> 16, of which waited for: 4 -> 6; matrix products, arithmetic and copies ran while one was open for 17% -> 4% of each run, Pallas kernels for 0% -> 0%
where the time goes in v1:
time: 186 us; the launch traced here: 183 us
  starting transfers between devices  75.9 us (41%)
  waiting for transfers between devices  44.5 us (24%)
  blocking collectives  42.9 us (23%)
  other arithmetic  7.27 us (4%)
  matrix products  5.19 us (3%)
  Pallas kernels  3.32 us (2%)
  local copies, waits for them, and re-layouts  2.57 us (1%)
    ppermute x13, starting transfers between devices, ring_shift(): lax.ppermute(value, axis, [(i, (i + step) % count) for i in range(count)])  47.4 us
    all_gather x1, blocking collectives, layer(): gathered = lax.all_gather(lifted, 'tensor', axis=0, tiled=True)  42.9 us
    ppermute x13, waiting for transfers between devices, ring_shift(): lax.ppermute(value, axis, [(i, (i + step) % count) for i in range(count)])  36.2 us
    ppermute x2, starting transfers between devices, swapped(): return wide(lax.ppermute(value, 'dp_1', [(0, 1), (1, 0)]))  20 us
    ppermute x1, starting transfers between devices, layer(): lax.ppermute(outgoing, 'section', [(s, s - 1) for s in range(1, sections)])  8.55 us
    ppermute x2, waiting for transfers between devices, swapped(): return wide(lax.ppermute(value, 'dp_1', [(0, 1), (1, 0)]))  7.44 us
  transfers between devices with their start and end apart: 16, of which 6 were waited for; matrix products, arithmetic and copies ran while one was open for 4% of the time, Pallas kernels for 0%

profile of v1, /device:TPU:1, one launch (start us, length us, event | category | flops | bytes accessed | tf_op | source)
XLA Modules:
  0.0 182.8 jit_solution(17701871489465053940)
XLA Ops:
  2.8 1.4 multiply_convert_fusion.4
  4.3 42.9 %all-gather.1 = f16[256,8192]{1,0:T(8,128)(2,1)S(1)} all-gather(f16[32,8192]{1,0:T(8,128)(2,1)S(1)} %multiply_convert_fusion.4), channel_id=1, replica_groups=mesh['section'=12,'tensor'=8,'dp_0'=4,'dp_1'=2] {'tensor'}, dimensions={0}, use_global_device_ids=true | all-gather | bytes 4718592 | tf_op jit(solution)/shard_map/all_gather | solution.py:170
  48.5 3.3 %attention_grads.1 = (bf16[2,128,1024]{2,1,0:T(8,128)(2,1)}, bf16[2,256,128]{2,1,0:T(8,128)(2,1)S(1)}, bf16[2,256,128]{2,1,0:T(8,128)(2,1)S(1)}) custom-call(s32[2]{0:T(128)S(1)} %bitcast.66, s32[2,128]{1,0:T(2,128)S(1)} %bitcast.65, bf16[2,256,128]{2,1,0:T(8,128)(2,1)S(1)} %fusion.10.pairs, bf16[2,128,1024]{2,1,0:T(8,128)(2,1)S(1)} %bitcast.63, ...), custom_call_target="tpu_custom_call" | custom-call | tf_op jit(solution)/shard_map/attention_grads/pallas_call | solution.py:100
  53.6 5.4 %collective-permute-start.11 = (bf16[2048,128]{1,0:T(8,128)(2,1)S(1)}, bf16[2048,128]{1,0:T(8,128)(2,1)S(1)}, u32[]{:S(2)}, u32[]{:S(2)}) collective-permute-start(bf16[2048,128]{1,0:T(8,128)(2,1)S(1)} %get-tuple-element.50), channel_id=1, source_target_pairs={{0,2},{2,4},{4,6},{6,0},{1,3},{3,5},{5,7},{7,1},{8,10},{10,12},{12... | collective-permute-start | bytes 1572872 | tf_op jit(solution)/shard_map/ppermute | solution.py:116
  60.4 2.3 %collective-permute-start = (bf16[32,8192]{1,0:T(8,128)(2,1)S(1)}, bf16[32,8192]{1,0:T(8,128)(2,1)S(1)}, u32[]{:S(2)}, u32[]{:S(2)}) collective-permute-start(bf16[32,8192]{1,0:T(8,128)(2,1)S(1)} %get-tuple-element.42), channel_id=1, source_target_pairs={{0,8},{8,16},{16,24},{24,32},{32,40},{40,48},{48,56},{56,0},{1,9},... | collective-permute-start | bytes 1572872 | tf_op jit(solution)/shard_map/ppermute | solution.py:116
  62.7 4.2 %collective-permute-start.3 = (bf16[32,8192]{1,0:T(8,128)(2,1)S(1)}, bf16[32,8192]{1,0:T(8,128)(2,1)S(1)}, u32[]{:S(2)}, u32[]{:S(2)}) collective-permute-start(bf16[32,8192]{1,0:T(8,128)(2,1)S(1)} %get-tuple-element.44), channel_id=1, source_target_pairs={{0,56},{8,0},{16,8},{24,16},{32,24},{40,32},{48,40},{56,48},{1,57}... | collective-permute-start | bytes 1572872 | tf_op jit(solution)/shard_map/ppermute | solution.py:116
  68.7 4.4 %collective-permute-start.10 = (bf16[2048,128]{1,0:T(8,128)(2,1)S(1)}, bf16[2048,128]{1,0:T(8,128)(2,1)S(1)}, u32[]{:S(2)}, u32[]{:S(2)}) collective-permute-start(bf16[2048,128]{1,0:T(8,128)(2,1)S(1)} %get-tuple-element.45), channel_id=1, source_target_pairs={{0,4},{2,6},{4,0},{6,2},{1,5},{3,7},{5,1},{7,3},{8,12},{10,14},{12... | collective-permute-start | bytes 1572872 | tf_op jit(solution)/shard_map/ppermute | solution.py:116
  73.0 3.1 %collective-permute-start.9 = (bf16[2048,128]{1,0:T(8,128)(2,1)S(1)}, bf16[2048,128]{1,0:T(8,128)(2,1)S(1)}, u32[]{:S(2)}, u32[]{:S(2)}) collective-permute-start(bf16[2048,128]{1,0:T(8,128)(2,1)S(1)} %get-tuple-element.46), channel_id=1, source_target_pairs={{0,6},{2,0},{4,2},{6,4},{1,7},{3,1},{5,3},{7,5},{8,14},{10,8},{12,... | collective-permute-start | bytes 1572872 | tf_op jit(solution)/shard_map/ppermute | solution.py:116
  76.1 2.2 %collective-permute-start.8 = (bf16[2048,128]{1,0:T(8,128)(2,1)S(1)}, bf16[2048,128]{1,0:T(8,128)(2,1)S(1)}, u32[]{:S(2)}, u32[]{:S(2)}) collective-permute-start(bf16[2048,128]{1,0:T(8,128)(2,1)S(1)} %get-tuple-element.47), channel_id=1, source_target_pairs={{0,2},{2,4},{4,6},{6,0},{1,3},{3,5},{5,7},{7,1},{8,10},{10,12},{12... | collective-permute-start | bytes 1572872 | tf_op jit(solution)/shard_map/ppermute | solution.py:116
  78.3 2.8 %collective-permute-start.13 = (bf16[2048,128]{1,0:T(8,128)(2,1)S(1)}, bf16[2048,128]{1,0:T(8,128)(2,1)S(1)}, u32[]{:S(2)}, u32[]{:S(2)}) collective-permute-start(bf16[2048,128]{1,0:T(8,128)(2,1)S(1)} %get-tuple-element.51), channel_id=1, source_target_pairs={{0,4},{2,6},{4,0},{6,2},{1,5},{3,7},{5,1},{7,3},{8,12},{10,14},{12... | collective-permute-start | bytes 1572872 | tf_op jit(solution)/shard_map/ppermute | solution.py:116
  81.2 3.4 %collective-permute-start.12 = (bf16[2048,128]{1,0:T(8,128)(2,1)S(1)}, bf16[2048,128]{1,0:T(8,128)(2,1)S(1)}, u32[]{:S(2)}, u32[]{:S(2)}) collective-permute-start(bf16[2048,128]{1,0:T(8,128)(2,1)S(1)} %get-tuple-element.52), channel_id=1, source_target_pairs={{0,6},{2,0},{4,2},{6,4},{1,7},{3,1},{5,3},{7,5},{8,14},{10,8},{12,... | collective-permute-start | bytes 1572872 | tf_op jit(solution)/shard_map/ppermute | solution.py:116
  84.8 19.1 %collective-permute-done.13 = bf16[2048,128]{1,0:T(8,128)(2,1)S(1)} collective-permute-done((bf16[2048,128]{1,0:T(8,128)(2,1)S(1)}, bf16[2048,128]{1,0:T(8,128)(2,1)S(1)}, u32[]{:S(2)}, u32[]{:S(2)}) %collective-permute-start.13) | collective-permute-done | bytes 524320 | tf_op jit(solution)/shard_map/ppermute | solution.py:116
  103.9 2.1 %collective-permute-start.1 = (bf16[32,8192]{1,0:T(8,128)(2,1)S(1)}, bf16[32,8192]{1,0:T(8,128)(2,1)S(1)}, u32[]{:S(2)}, u32[]{:S(2)}) collective-permute-start(bf16[32,8192]{1,0:T(8,128)(2,1)S(1)} %get-tuple-element.40), channel_id=1, source_target_pairs={{0,8},{8,16},{16,24},{24,32},{32,40},{40,48},{48,56},{56,0},{1,9},... | collective-permute-start | bytes 1572872 | tf_op jit(solution)/shard_map/ppermute | solution.py:116
  106.1 8.6 %collective-permute-done.12 = bf16[2048,128]{1,0:T(8,128)(2,1)S(1)} collective-permute-done((bf16[2048,128]{1,0:T(8,128)(2,1)S(1)}, bf16[2048,128]{1,0:T(8,128)(2,1)S(1)}, u32[]{:S(2)}, u32[]{:S(2)}) %collective-permute-start.12) | collective-permute-done | bytes 524320 | tf_op jit(solution)/shard_map/ppermute | solution.py:116
  114.7 3.0 %collective-permute-start.4 = (bf16[32,8192]{1,0:T(8,128)(2,1)S(1)}, bf16[32,8192]{1,0:T(8,128)(2,1)S(1)}, u32[]{:S(2)}, u32[]{:S(2)}) collective-permute-start(bf16[32,8192]{1,0:T(8,128)(2,1)S(1)} %get-tuple-element.41), channel_id=1, source_target_pairs={{0,56},{8,0},{16,8},{24,16},{32,24},{40,32},{48,40},{56,48},{1,57}... | collective-permute-start | bytes 1572872 | tf_op jit(solution)/shard_map/ppermute | solution.py:116
  118.2 7.8 %collective-permute-start.6 = (bf16[32,8192]{1,0:T(8,128)(2,1)S(1)}, bf16[32,8192]{1,0:T(8,128)(2,1)S(1)}, u32[]{:S(2)}, u32[]{:S(2)}) collective-permute-start(bf16[32,8192]{1,0:T(8,128)(2,1)S(1)} %get-tuple-element.43), channel_id=1, source_target_pairs={{0,32},{8,40},{16,48},{24,56},{32,0},{40,8},{48,16},{56,24},{1,33}... | collective-permute-start | bytes 1572872 | tf_op jit(solution)/shard_map/ppermute | solution.py:116
  126.2 15.0 %collective-permute-start.14 = (bf16[1024,128]{1,0:T(8,128)(2,1)S(1)}, bf16[1024,128]{1,0:T(8,128)(2,1)S(1)}, u32[]{:S(2)}, u32[]{:S(2)}) collective-permute-start(bf16[1024,128]{1,0:T(8,128)(2,1)S(1)} %select_convert_fusion), channel_id=1, source_target_pairs={{0,1},{1,0},{2,3},{3,2},{4,5},{5,4},{6,7},{7,6},{8,9},{9,8},{10,11... | collective-permute-start | bytes 786440 | tf_op jit(solution)/shard_map/ppermute | solution.py:142
  141.6 3.4 %collective-permute-start.2 = (bf16[32,8192]{1,0:T(8,128)(2,1)S(1)}, bf16[32,8192]{1,0:T(8,128)(2,1)S(1)}, u32[]{:S(2)}, u32[]{:S(2)}) collective-permute-start(bf16[32,8192]{1,0:T(8,128)(2,1)S(1)} %get-tuple-element.38), channel_id=1, source_target_pairs={{0,8},{8,16},{16,24},{24,32},{32,40},{40,48},{48,56},{56,0},{1,9},... | collective-permute-start | bytes 1572872 | tf_op jit(solution)/shard_map/ppermute | solution.py:116
  144.9 3.4 %collective-permute-start.5 = (bf16[32,8192]{1,0:T(8,128)(2,1)S(1)}, bf16[32,8192]{1,0:T(8,128)(2,1)S(1)}, u32[]{:S(2)}, u32[]{:S(2)}) collective-permute-start(bf16[32,8192]{1,0:T(8,128)(2,1)S(1)} %get-tuple-element.39), channel_id=1, source_target_pairs={{0,56},{8,0},{16,8},{24,16},{32,24},{40,32},{48,40},{56,48},{1,57}... | collective-permute-start | bytes 1572872 | tf_op jit(solution)/shard_map/ppermute | solution.py:116
  148.4 5.0 %collective-permute-start.15 = (bf16[1024,128]{1,0:T(8,128)(2,1)S(1)}, bf16[1024,128]{1,0:T(8,128)(2,1)S(1)}, u32[]{:S(2)}, u32[]{:S(2)}) collective-permute-start(bf16[1024,128]{1,0:T(8,128)(2,1)S(1)} %select_convert_fusion.1), channel_id=1, source_target_pairs={{0,1},{1,0},{2,3},{3,2},{4,5},{5,4},{6,7},{7,6},{8,9},{9,8},{10,11... | collective-permute-start | bytes 786440 | tf_op jit(solution)/shard_map/ppermute | solution.py:142
  153.7 5.3 %collective-permute-done.2 = bf16[32,8192]{1,0:T(8,128)(2,1)S(1)} collective-permute-done((bf16[32,8192]{1,0:T(8,128)(2,1)S(1)}, bf16[32,8192]{1,0:T(8,128)(2,1)S(1)}, u32[]{:S(2)}, u32[]{:S(2)}) %collective-permute-start.2) | collective-permute-done | bytes 524320 | tf_op jit(solution)/shard_map/ppermute | solution.py:116
  159.0 3.2 %collective-permute-done.5 = bf16[32,8192]{1,0:T(8,128)(2,1)S(1)} collective-permute-done((bf16[32,8192]{1,0:T(8,128)(2,1)S(1)}, bf16[32,8192]{1,0:T(8,128)(2,1)S(1)}, u32[]{:S(2)}, u32[]{:S(2)}) %collective-permute-start.5) | collective-permute-done | bytes 524320 | tf_op jit(solution)/shard_map/ppermute | solution.py:116
  163.3 8.5 %collective-permute-start.7 = (bf16[16,8192]{1,0:T(8,128)(2,1)S(1)}, bf16[16,8192]{1,0:T(8,128)(2,1)S(1)}, u32[]{:S(2)}, u32[]{:S(2)}) collective-permute-start(bf16[16,8192]{1,0:T(8,128)(2,1)S(1)} %fusion.24), channel_id=1, source_target_pairs={{64,0},{128,64},{192,128},{256,192},{320,256},{384,320},{448,384},... | collective-permute-start | bytes 786440 | tf_op jit(solution)/shard_map/ppermute | solution.py:220
  171.9 7.4 %collective-permute-done.15 = bf16[1024,128]{1,0:T(8,128)(2,1)S(1)} collective-permute-done((bf16[1024,128]{1,0:T(8,128)(2,1)S(1)}, bf16[1024,128]{1,0:T(8,128)(2,1)S(1)}, u32[]{:S(2)}, u32[]{:S(2)}) %collective-permute-start.15) | collective-permute-done | bytes 262176 | tf_op jit(solution)/shard_map/ppermute | solution.py:142
  (52 shorter events, 14.5 us)
Async XLA Ops:
  2.8 44.4 %copy-start.5 = (bf16[1,8192,1,2,128]{4,3,2,1,0:T(2,128)(2,1)S(1)}, bf16[1,8192,1,2,128]{4,3,2,1,0:T(2,128)(2,1)}, u32[]{:S(2)}) copy-start(bf16[1,8192,1,2,128]{4,3,2,1,0:T(2,128)(2,1)} %param.11) | copy-start | bytes 12582916
  47.2 1.3 copy-start
  47.2 1.3 copy-start.1
  47.2 1.3 copy-start.2
  47.2 1.3 copy-start.3
  53.6 22.5 %collective-permute-start.11 = (bf16[2048,128]{1,0:T(8,128)(2,1)S(1)}, bf16[2048,128]{1,0:T(8,128)(2,1)S(1)}, u32[]{:S(2)}, u32[]{:S(2)}) collective-permute-start(bf16[2048,128]{1,0:T(8,128)(2,1)S(1)} %get-tuple-element.50), channel_id=1, source_target_pairs={{0,2},{2,4},{4,6},{6,0},{1,3},{3,5},{5,7},{7,1},{8,10},{10,12},{12... | collective-permute-start | bytes 1572872 | tf_op jit(solution)/shard_map/ppermute | solution.py:116
  60.4 17.9 %collective-permute-start = (bf16[32,8192]{1,0:T(8,128)(2,1)S(1)}, bf16[32,8192]{1,0:T(8,128)(2,1)S(1)}, u32[]{:S(2)}, u32[]{:S(2)}) collective-permute-start(bf16[32,8192]{1,0:T(8,128)(2,1)S(1)} %get-tuple-element.42), channel_id=1, source_target_pairs={{0,8},{8,16},{16,24},{24,32},{32,40},{40,48},{48,56},{56,0},{1,9},... | collective-permute-start | bytes 1572872 | tf_op jit(solution)/shard_map/ppermute | solution.py:116
  62.7 18.4 %collective-permute-start.3 = (bf16[32,8192]{1,0:T(8,128)(2,1)S(1)}, bf16[32,8192]{1,0:T(8,128)(2,1)S(1)}, u32[]{:S(2)}, u32[]{:S(2)}) collective-permute-start(bf16[32,8192]{1,0:T(8,128)(2,1)S(1)} %get-tuple-element.44), channel_id=1, source_target_pairs={{0,56},{8,0},{16,8},{24,16},{32,24},{40,32},{48,40},{56,48},{1,57}... | collective-permute-start | bytes 1572872 | tf_op jit(solution)/shard_map/ppermute | solution.py:116
  68.7 49.5 %collective-permute-start.10 = (bf16[2048,128]{1,0:T(8,128)(2,1)S(1)}, bf16[2048,128]{1,0:T(8,128)(2,1)S(1)}, u32[]{:S(2)}, u32[]{:S(2)}) collective-permute-start(bf16[2048,128]{1,0:T(8,128)(2,1)S(1)} %get-tuple-element.45), channel_id=1, source_target_pairs={{0,4},{2,6},{4,0},{6,2},{1,5},{3,7},{5,1},{7,3},{8,12},{10,14},{12... | collective-permute-start | bytes 1572872 | tf_op jit(solution)/shard_map/ppermute | solution.py:116
  73.0 52.9 %collective-permute-start.9 = (bf16[2048,128]{1,0:T(8,128)(2,1)S(1)}, bf16[2048,128]{1,0:T(8,128)(2,1)S(1)}, u32[]{:S(2)}, u32[]{:S(2)}) collective-permute-start(bf16[2048,128]{1,0:T(8,128)(2,1)S(1)} %get-tuple-element.46), channel_id=1, source_target_pairs={{0,6},{2,0},{4,2},{6,4},{1,7},{3,1},{5,3},{7,5},{8,14},{10,8},{12,... | collective-permute-start | bytes 1572872 | tf_op jit(solution)/shard_map/ppermute | solution.py:116
  76.1 49.8 %collective-permute-start.8 = (bf16[2048,128]{1,0:T(8,128)(2,1)S(1)}, bf16[2048,128]{1,0:T(8,128)(2,1)S(1)}, u32[]{:S(2)}, u32[]{:S(2)}) collective-permute-start(bf16[2048,128]{1,0:T(8,128)(2,1)S(1)} %get-tuple-element.47), channel_id=1, source_target_pairs={{0,2},{2,4},{4,6},{6,0},{1,3},{3,5},{5,7},{7,1},{8,10},{10,12},{12... | collective-permute-start | bytes 1572872 | tf_op jit(solution)/shard_map/ppermute | solution.py:116
  78.3 25.6 %collective-permute-start.13 = (bf16[2048,128]{1,0:T(8,128)(2,1)S(1)}, bf16[2048,128]{1,0:T(8,128)(2,1)S(1)}, u32[]{:S(2)}, u32[]{:S(2)}) collective-permute-start(bf16[2048,128]{1,0:T(8,128)(2,1)S(1)} %get-tuple-element.51), channel_id=1, source_target_pairs={{0,4},{2,6},{4,0},{6,2},{1,5},{3,7},{5,1},{7,3},{8,12},{10,14},{12... | collective-permute-start | bytes 1572872 | tf_op jit(solution)/shard_map/ppermute | solution.py:116
  81.2 33.5 %collective-permute-start.12 = (bf16[2048,128]{1,0:T(8,128)(2,1)S(1)}, bf16[2048,128]{1,0:T(8,128)(2,1)S(1)}, u32[]{:S(2)}, u32[]{:S(2)}) collective-permute-start(bf16[2048,128]{1,0:T(8,128)(2,1)S(1)} %get-tuple-element.52), channel_id=1, source_target_pairs={{0,6},{2,0},{4,2},{6,4},{1,7},{3,1},{5,3},{7,5},{8,14},{10,8},{12,... | collective-permute-start | bytes 1572872 | tf_op jit(solution)/shard_map/ppermute | solution.py:116
  103.9 37.4 %collective-permute-start.1 = (bf16[32,8192]{1,0:T(8,128)(2,1)S(1)}, bf16[32,8192]{1,0:T(8,128)(2,1)S(1)}, u32[]{:S(2)}, u32[]{:S(2)}) collective-permute-start(bf16[32,8192]{1,0:T(8,128)(2,1)S(1)} %get-tuple-element.40), channel_id=1, source_target_pairs={{0,8},{8,16},{16,24},{24,32},{32,40},{40,48},{48,56},{56,0},{1,9},... | collective-permute-start | bytes 1572872 | tf_op jit(solution)/shard_map/ppermute | solution.py:116
  114.7 26.6 %collective-permute-start.4 = (bf16[32,8192]{1,0:T(8,128)(2,1)S(1)}, bf16[32,8192]{1,0:T(8,128)(2,1)S(1)}, u32[]{:S(2)}, u32[]{:S(2)}) collective-permute-start(bf16[32,8192]{1,0:T(8,128)(2,1)S(1)} %get-tuple-element.41), channel_id=1, source_target_pairs={{0,56},{8,0},{16,8},{24,16},{32,24},{40,32},{48,40},{56,48},{1,57}... | collective-permute-start | bytes 1572872 | tf_op jit(solution)/shard_map/ppermute | solution.py:116
  118.1 44.1 %copy-start.4 = (bf16[1,1,2,16,8192]{4,3,2,1,0:T(8,128)(2,1)S(1)}, bf16[1,1,2,16,8192]{4,3,2,1,0:T(8,128)(2,1)}, u32[]{:S(2)}) copy-start(bf16[1,1,2,16,8192]{4,3,2,1,0:T(8,128)(2,1)} %param.9) | copy-start | bytes 1572868
  118.2 35.5 %collective-permute-start.6 = (bf16[32,8192]{1,0:T(8,128)(2,1)S(1)}, bf16[32,8192]{1,0:T(8,128)(2,1)S(1)}, u32[]{:S(2)}, u32[]{:S(2)}) collective-permute-start(bf16[32,8192]{1,0:T(8,128)(2,1)S(1)} %get-tuple-element.43), channel_id=1, source_target_pairs={{0,32},{8,40},{16,48},{24,56},{32,0},{40,8},{48,16},{56,24},{1,33}... | collective-permute-start | bytes 1572872 | tf_op jit(solution)/shard_map/ppermute | solution.py:116
  126.2 27.1 %collective-permute-start.14 = (bf16[1024,128]{1,0:T(8,128)(2,1)S(1)}, bf16[1024,128]{1,0:T(8,128)(2,1)S(1)}, u32[]{:S(2)}, u32[]{:S(2)}) collective-permute-start(bf16[1024,128]{1,0:T(8,128)(2,1)S(1)} %select_convert_fusion), channel_id=1, source_target_pairs={{0,1},{1,0},{2,3},{3,2},{4,5},{5,4},{6,7},{7,6},{8,9},{9,8},{10,11... | collective-permute-start | bytes 786440 | tf_op jit(solution)/shard_map/ppermute | solution.py:142
  141.6 17.4 %collective-permute-start.2 = (bf16[32,8192]{1,0:T(8,128)(2,1)S(1)}, bf16[32,8192]{1,0:T(8,128)(2,1)S(1)}, u32[]{:S(2)}, u32[]{:S(2)}) collective-permute-start(bf16[32,8192]{1,0:T(8,128)(2,1)S(1)} %get-tuple-element.38), channel_id=1, source_target_pairs={{0,8},{8,16},{16,24},{24,32},{32,40},{40,48},{48,56},{56,0},{1,9},... | collective-permute-start | bytes 1572872 | tf_op jit(solution)/shard_map/ppermute | solution.py:116
  144.9 18.3 %copy-start.7 = (bf16[1,1,16,8192]{3,2,1,0:T(8,128)(2,1)S(1)}, bf16[1,1,16,8192]{3,2,1,0:T(8,128)(2,1)}, u32[]{:S(2)}) copy-start(bf16[1,1,16,8192]{3,2,1,0:T(8,128)(2,1)} %param.14) | copy-start | bytes 786436
  144.9 17.3 %collective-permute-start.5 = (bf16[32,8192]{1,0:T(8,128)(2,1)S(1)}, bf16[32,8192]{1,0:T(8,128)(2,1)S(1)}, u32[]{:S(2)}, u32[]{:S(2)}) collective-permute-start(bf16[32,8192]{1,0:T(8,128)(2,1)S(1)} %get-tuple-element.39), channel_id=1, source_target_pairs={{0,56},{8,0},{16,8},{24,16},{32,24},{40,32},{48,40},{56,48},{1,57}... | collective-permute-start | bytes 1572872 | tf_op jit(solution)/shard_map/ppermute | solution.py:116
  148.4 30.9 %collective-permute-start.15 = (bf16[1024,128]{1,0:T(8,128)(2,1)S(1)}, bf16[1024,128]{1,0:T(8,128)(2,1)S(1)}, u32[]{:S(2)}, u32[]{:S(2)}) collective-permute-start(bf16[1024,128]{1,0:T(8,128)(2,1)S(1)} %select_convert_fusion.1), channel_id=1, source_target_pairs={{0,1},{1,0},{2,3},{3,2},{4,5},{5,4},{6,7},{7,6},{8,9},{9,8},{10,11... | collective-permute-start | bytes 786440 | tf_op jit(solution)/shard_map/ppermute | solution.py:142
  162.7 19.3 %copy-start.6 = (bf16[1,16,8192]{2,1,0:T(8,128)(2,1)S(1)}, bf16[1,16,8192]{2,1,0:T(8,128)(2,1)}, u32[]{:S(2)}) copy-start(bf16[1,16,8192]{2,1,0:T(8,128)(2,1)} %param.15) | copy-start | bytes 786436
  163.3 18.7 %collective-permute-start.7 = (bf16[16,8192]{1,0:T(8,128)(2,1)S(1)}, bf16[16,8192]{1,0:T(8,128)(2,1)S(1)}, u32[]{:S(2)}, u32[]{:S(2)}) collective-permute-start(bf16[16,8192]{1,0:T(8,128)(2,1)S(1)} %fusion.24), channel_id=1, source_target_pairs={{64,0},{128,64},{192,128},{256,192},{320,256},{384,320},{448,384},... | collective-permute-start | bytes 786440 | tf_op jit(solution)/shard_map/ppermute | solution.py:220

commit v2 on v1

--- a/solution.py
+++ b/solution.py
@@ -198,14 +198,14 @@
     parts_k = replica_parts(replica_term(0), own)
     parts_k, _ = lax.optimization_barrier((parts_k, sent_v))
     sent_k, kept_k = replica_sum(parts_k, upper)
-    across = ring_shift(term(4), "tensor", 4)
-    up = ring_shift(term(3), "tensor", 1)
+    up = ring_shift(term(4), "tensor", 1)
+    up = ring_shift(plus(up, term(3)), "tensor", 1)
     down = ring_shift(term(-3), "tensor", -1)
     up = ring_shift(plus(up, term(2)), "tensor", 1)
     down = ring_shift(plus(down, term(-2)), "tensor", -1)
     up = ring_shift(plus(up, term(1)), "tensor", 1)
     down = ring_shift(plus(down, term(-1)), "tensor", -1)
-    normed_grad = wide(term(0)) + wide(up) + wide(down) + wide(across)
+    normed_grad = wide(term(0)) + wide(up) + wide(down)
 
     values_total = low(kept_v + swapped(sent_v))
     keys_total = low(kept_k + swapped(sent_k))

time: 186 us -> 188 us (1.011); the launches traced: 183 us -> 188 us
  waiting for transfers between devices: 44.5 us -> 47.3 us
  starting transfers between devices: 75.9 us -> 78 us
    ppermute x2, waiting for transfers between devices: 7.44 us -> 17.5 us  [swapped(): return wide(lax.ppermute(value, 'dp_1', [(0, 1), (1, 0)]))]
    ppermute x13, waiting for transfers between devices: 36.2 us -> 29.8 us  [ring_shift(): lax.ppermute(value, axis, [(i, (i + step) % count) for i in range(count)])]
    ppermute x2, starting transfers between devices: 20 us -> 24.4 us  [swapped(): return wide(lax.ppermute(value, 'dp_1', [(0, 1), (1, 0)]))]
    ppermute x1, starting transfers between devices: 8.55 us -> 4.93 us  [layer(): lax.ppermute(outgoing, 'section', [(s, s - 1) for s in range(1, sections)])]
  transfers between devices with their start and end apart: 16 -> 16, of which waited for: 6 -> 3; matrix products, arithmetic and copies ran while one was open for 4% -> 4% of each run, Pallas kernels for 0% -> 0%
where the time goes in v2:
time: 188 us
  starting transfers between devices  78 us (41%)
  waiting for transfers between devices  47.3 us (25%)
  blocking collectives  42.9 us (23%)
  other arithmetic  7.27 us (4%)
  matrix products  5.2 us (3%)
  Pallas kernels  3.32 us (2%)
  local copies, waits for them, and re-layouts  2.53 us (1%)
    ppermute x13, starting transfers between devices, ring_shift(): lax.ppermute(value, axis, [(i, (i + step) % count) for i in range(count)])  48.7 us
    all_gather x1, blocking collectives, layer(): gathered = lax.all_gather(lifted, 'tensor', axis=0, tiled=True)  42.9 us
    ppermute x13, waiting for transfers between devices, ring_shift(): lax.ppermute(value, axis, [(i, (i + step) % count) for i in range(count)])  29.8 us
    ppermute x2, starting transfers between devices, swapped(): return wide(lax.ppermute(value, 'dp_1', [(0, 1), (1, 0)]))  24.4 us
    ppermute x2, waiting for transfers between devices, swapped(): return wide(lax.ppermute(value, 'dp_1', [(0, 1), (1, 0)]))  17.5 us
    ppermute x1, starting transfers between devices, layer(): lax.ppermute(outgoing, 'section', [(s, s - 1) for s in range(1, sections)])  4.93 us
  transfers between devices with their start and end apart: 16, of which 3 were waited for; matrix products, arithmetic and copies ran while one was open for 4% of the time, Pallas kernels for 0%

profile of v2, /device:TPU:1, one launch (start us, length us, event | category | flops | bytes accessed | tf_op | source)
XLA Modules:
  0.0 187.6 jit_solution(11326766323118549346)
XLA Ops:
  2.8 1.4 multiply_convert_fusion.4
  4.3 42.9 %all-gather.1 = f16[256,8192]{1,0:T(8,128)(2,1)S(1)} all-gather(f16[32,8192]{1,0:T(8,128)(2,1)S(1)} %multiply_convert_fusion.4), channel_id=1, replica_groups=mesh['section'=12,'tensor'=8,'dp_0'=4,'dp_1'=2] {'tensor'}, dimensions={0}, use_global_device_ids=true | all-gather | bytes 4718592 | tf_op jit(solution)/shard_map/all_gather | solution.py:170
  48.5 3.3 %attention_grads.1 = (bf16[2,128,1024]{2,1,0:T(8,128)(2,1)}, bf16[2,256,128]{2,1,0:T(8,128)(2,1)S(1)}, bf16[2,256,128]{2,1,0:T(8,128)(2,1)S(1)}) custom-call(s32[2]{0:T(128)S(1)} %bitcast.66, s32[2,128]{1,0:T(2,128)S(1)} %bitcast.65, bf16[2,256,128]{2,1,0:T(8,128)(2,1)S(1)} %fusion.10.pairs, bf16[2,128,1024]{2,1,0:T(8,128)(2,1)S(1)} %bitcast.63, ...), custom_call_target="tpu_custom_call" | custom-call | tf_op jit(solution)/shard_map/attention_grads/pallas_call | solution.py:100
  53.2 3.2 %collective-permute-start = (bf16[32,8192]{1,0:T(8,128)(2,1)S(1)}, bf16[32,8192]{1,0:T(8,128)(2,1)S(1)}, u32[]{:S(2)}, u32[]{:S(2)}) collective-permute-start(bf16[32,8192]{1,0:T(8,128)(2,1)S(1)} %get-tuple-element.42), channel_id=1, source_target_pairs={{0,8},{8,16},{16,24},{24,32},{32,40},{40,48},{48,56},{56,0},{1,9},... | collective-permute-start | bytes 1572872 | tf_op jit(solution)/shard_map/ppermute | solution.py:116
  58.2 4.4 %collective-permute-start.11 = (bf16[2048,128]{1,0:T(8,128)(2,1)S(1)}, bf16[2048,128]{1,0:T(8,128)(2,1)S(1)}, u32[]{:S(2)}, u32[]{:S(2)}) collective-permute-start(bf16[2048,128]{1,0:T(8,128)(2,1)S(1)} %get-tuple-element.49), channel_id=1, source_target_pairs={{0,2},{2,4},{4,6},{6,0},{1,3},{3,5},{5,7},{7,1},{8,10},{10,12},{12... | collective-permute-start | bytes 1572872 | tf_op jit(solution)/shard_map/ppermute | solution.py:116
  62.7 4.2 %collective-permute-start.4 = (bf16[32,8192]{1,0:T(8,128)(2,1)S(1)}, bf16[32,8192]{1,0:T(8,128)(2,1)S(1)}, u32[]{:S(2)}, u32[]{:S(2)}) collective-permute-start(bf16[32,8192]{1,0:T(8,128)(2,1)S(1)} %get-tuple-element.43), channel_id=1, source_target_pairs={{0,56},{8,0},{16,8},{24,16},{32,24},{40,32},{48,40},{56,48},{1,57}... | collective-permute-start | bytes 1572872 | tf_op jit(solution)/shard_map/ppermute | solution.py:116
  67.0 1.9 %collective-permute-start.1 = (bf16[32,8192]{1,0:T(8,128)(2,1)S(1)}, bf16[32,8192]{1,0:T(8,128)(2,1)S(1)}, u32[]{:S(2)}, u32[]{:S(2)}) collective-permute-start(bf16[32,8192]{1,0:T(8,128)(2,1)S(1)} %add_convert_fusion.4), channel_id=1, source_target_pairs={{0,8},{8,16},{16,24},{24,32},{32,40},{40,48},{48,56},{56,0},{1,9},... | collective-permute-start | bytes 1572872 | tf_op jit(solution)/shard_map/ppermute | solution.py:116
  68.9 1.3 convolution_convert_fusion.1
  70.7 8.3 %collective-permute-start.10 = (bf16[2048,128]{1,0:T(8,128)(2,1)S(1)}, bf16[2048,128]{1,0:T(8,128)(2,1)S(1)}, u32[]{:S(2)}, u32[]{:S(2)}) collective-permute-start(bf16[2048,128]{1,0:T(8,128)(2,1)S(1)} %get-tuple-element.44), channel_id=1, source_target_pairs={{0,4},{2,6},{4,0},{6,2},{1,5},{3,7},{5,1},{7,3},{8,12},{10,14},{12... | collective-permute-start | bytes 1572872 | tf_op jit(solution)/shard_map/ppermute | solution.py:116
  79.0 2.8 %collective-permute-start.9 = (bf16[2048,128]{1,0:T(8,128)(2,1)S(1)}, bf16[2048,128]{1,0:T(8,128)(2,1)S(1)}, u32[]{:S(2)}, u32[]{:S(2)}) collective-permute-start(bf16[2048,128]{1,0:T(8,128)(2,1)S(1)} %get-tuple-element.45), channel_id=1, source_target_pairs={{0,6},{2,0},{4,2},{6,4},{1,7},{3,1},{5,3},{7,5},{8,14},{10,8},{12,... | collective-permute-start | bytes 1572872 | tf_op jit(solution)/shard_map/ppermute | solution.py:116
  81.8 2.5 %collective-permute-start.8 = (bf16[2048,128]{1,0:T(8,128)(2,1)S(1)}, bf16[2048,128]{1,0:T(8,128)(2,1)S(1)}, u32[]{:S(2)}, u32[]{:S(2)}) collective-permute-start(bf16[2048,128]{1,0:T(8,128)(2,1)S(1)} %get-tuple-element.46), channel_id=1, source_target_pairs={{0,2},{2,4},{4,6},{6,0},{1,3},{3,5},{5,7},{7,1},{8,10},{10,12},{12... | collective-permute-start | bytes 1572872 | tf_op jit(solution)/shard_map/ppermute | solution.py:116
  84.3 2.5 %collective-permute-start.13 = (bf16[2048,128]{1,0:T(8,128)(2,1)S(1)}, bf16[2048,128]{1,0:T(8,128)(2,1)S(1)}, u32[]{:S(2)}, u32[]{:S(2)}) collective-permute-start(bf16[2048,128]{1,0:T(8,128)(2,1)S(1)} %get-tuple-element.50), channel_id=1, source_target_pairs={{0,4},{2,6},{4,0},{6,2},{1,5},{3,7},{5,1},{7,3},{8,12},{10,14},{12... | collective-permute-start | bytes 1572872 | tf_op jit(solution)/shard_map/ppermute | solution.py:116
  86.9 4.0 %collective-permute-start.12 = (bf16[2048,128]{1,0:T(8,128)(2,1)S(1)}, bf16[2048,128]{1,0:T(8,128)(2,1)S(1)}, u32[]{:S(2)}, u32[]{:S(2)}) collective-permute-start(bf16[2048,128]{1,0:T(8,128)(2,1)S(1)} %get-tuple-element.51), channel_id=1, source_target_pairs={{0,6},{2,0},{4,2},{6,4},{1,7},{3,1},{5,3},{7,5},{8,14},{10,8},{12,... | collective-permute-start | bytes 1572872 | tf_op jit(solution)/shard_map/ppermute | solution.py:116
  91.1 19.3 %collective-permute-done.13 = bf16[2048,128]{1,0:T(8,128)(2,1)S(1)} collective-permute-done((bf16[2048,128]{1,0:T(8,128)(2,1)S(1)}, bf16[2048,128]{1,0:T(8,128)(2,1)S(1)}, u32[]{:S(2)}, u32[]{:S(2)}) %collective-permute-start.13) | collective-permute-done | bytes 524320 | tf_op jit(solution)/shard_map/ppermute | solution.py:116
  110.4 3.5 %collective-permute-start.2 = (bf16[32,8192]{1,0:T(8,128)(2,1)S(1)}, bf16[32,8192]{1,0:T(8,128)(2,1)S(1)}, u32[]{:S(2)}, u32[]{:S(2)}) collective-permute-start(bf16[32,8192]{1,0:T(8,128)(2,1)S(1)} %get-tuple-element.40), channel_id=1, source_target_pairs={{0,8},{8,16},{16,24},{24,32},{32,40},{40,48},{48,56},{56,0},{1,9},... | collective-permute-start | bytes 1572872 | tf_op jit(solution)/shard_map/ppermute | solution.py:116
  113.9 10.5 %collective-permute-done.12 = bf16[2048,128]{1,0:T(8,128)(2,1)S(1)} collective-permute-done((bf16[2048,128]{1,0:T(8,128)(2,1)S(1)}, bf16[2048,128]{1,0:T(8,128)(2,1)S(1)}, u32[]{:S(2)}, u32[]{:S(2)}) %collective-permute-start.12) | collective-permute-done | bytes 524320 | tf_op jit(solution)/shard_map/ppermute | solution.py:116
  124.3 4.6 %collective-permute-start.5 = (bf16[32,8192]{1,0:T(8,128)(2,1)S(1)}, bf16[32,8192]{1,0:T(8,128)(2,1)S(1)}, u32[]{:S(2)}, u32[]{:S(2)}) collective-permute-start(bf16[32,8192]{1,0:T(8,128)(2,1)S(1)} %get-tuple-element.41), channel_id=1, source_target_pairs={{0,56},{8,0},{16,8},{24,16},{32,24},{40,32},{48,40},{56,48},{1,57}... | collective-permute-start | bytes 1572872 | tf_op jit(solution)/shard_map/ppermute | solution.py:116
  129.7 14.9 %collective-permute-start.14 = (bf16[1024,128]{1,0:T(8,128)(2,1)S(1)}, bf16[1024,128]{1,0:T(8,128)(2,1)S(1)}, u32[]{:S(2)}, u32[]{:S(2)}) collective-permute-start(bf16[1024,128]{1,0:T(8,128)(2,1)S(1)} %select_convert_fusion), channel_id=1, source_target_pairs={{0,1},{1,0},{2,3},{3,2},{4,5},{5,4},{6,7},{7,6},{8,9},{9,8},{10,11... | collective-permute-start | bytes 786440 | tf_op jit(solution)/shard_map/ppermute | solution.py:142
  144.9 2.1 %collective-permute-start.3 = (bf16[32,8192]{1,0:T(8,128)(2,1)S(1)}, bf16[32,8192]{1,0:T(8,128)(2,1)S(1)}, u32[]{:S(2)}, u32[]{:S(2)}) collective-permute-start(bf16[32,8192]{1,0:T(8,128)(2,1)S(1)} %get-tuple-element.38), channel_id=1, source_target_pairs={{0,8},{8,16},{16,24},{24,32},{32,40},{40,48},{48,56},{56,0},{1,9},... | collective-permute-start | bytes 1572872 | tf_op jit(solution)/shard_map/ppermute | solution.py:116
  147.0 4.8 %collective-permute-start.6 = (bf16[32,8192]{1,0:T(8,128)(2,1)S(1)}, bf16[32,8192]{1,0:T(8,128)(2,1)S(1)}, u32[]{:S(2)}, u32[]{:S(2)}) collective-permute-start(bf16[32,8192]{1,0:T(8,128)(2,1)S(1)} %get-tuple-element.39), channel_id=1, source_target_pairs={{0,56},{8,0},{16,8},{24,16},{32,24},{40,32},{48,40},{56,48},{1,57}... | collective-permute-start | bytes 1572872 | tf_op jit(solution)/shard_map/ppermute | solution.py:116
  151.7 9.5 %collective-permute-start.15 = (bf16[1024,128]{1,0:T(8,128)(2,1)S(1)}, bf16[1024,128]{1,0:T(8,128)(2,1)S(1)}, u32[]{:S(2)}, u32[]{:S(2)}) collective-permute-start(bf16[1024,128]{1,0:T(8,128)(2,1)S(1)} %select_convert_fusion.1), channel_id=1, source_target_pairs={{0,1},{1,0},{2,3},{3,2},{4,5},{5,4},{6,7},{7,6},{8,9},{9,8},{10,11... | collective-permute-start | bytes 786440 | tf_op jit(solution)/shard_map/ppermute | solution.py:142
  162.6 4.9 %collective-permute-start.7 = (bf16[16,8192]{1,0:T(8,128)(2,1)S(1)}, bf16[16,8192]{1,0:T(8,128)(2,1)S(1)}, u32[]{:S(2)}, u32[]{:S(2)}) collective-permute-start(bf16[16,8192]{1,0:T(8,128)(2,1)S(1)} %fusion.24), channel_id=1, source_target_pairs={{64,0},{128,64},{192,128},{256,192},{320,256},{384,320},{448,384},... | collective-permute-start | bytes 786440 | tf_op jit(solution)/shard_map/ppermute | solution.py:220
  167.6 17.5 %collective-permute-done.15 = bf16[1024,128]{1,0:T(8,128)(2,1)S(1)} collective-permute-done((bf16[1024,128]{1,0:T(8,128)(2,1)S(1)}, bf16[1024,128]{1,0:T(8,128)(2,1)S(1)}, u32[]{:S(2)}, u32[]{:S(2)}) %collective-permute-start.15) | collective-permute-done | bytes 262176 | tf_op jit(solution)/shard_map/ppermute | solution.py:142
  185.5 1.3 copy.15
  (53 shorter events, 10.9 us)
Async XLA Ops:
  2.8 44.4 %copy-start.5 = (bf16[1,8192,1,2,128]{4,3,2,1,0:T(2,128)(2,1)S(1)}, bf16[1,8192,1,2,128]{4,3,2,1,0:T(2,128)(2,1)}, u32[]{:S(2)}) copy-start(bf16[1,8192,1,2,128]{4,3,2,1,0:T(2,128)(2,1)} %param.11) | copy-start | bytes 12582916
  47.2 1.3 copy-start
  47.2 1.3 copy-start.1
  47.2 1.3 copy-start.2
  47.2 1.3 copy-start.3
  53.2 13.6 %collective-permute-start = (bf16[32,8192]{1,0:T(8,128)(2,1)S(1)}, bf16[32,8192]{1,0:T(8,128)(2,1)S(1)}, u32[]{:S(2)}, u32[]{:S(2)}) collective-permute-start(bf16[32,8192]{1,0:T(8,128)(2,1)S(1)} %get-tuple-element.42), channel_id=1, source_target_pairs={{0,8},{8,16},{16,24},{24,32},{32,40},{40,48},{48,56},{56,0},{1,9},... | collective-permute-start | bytes 1572872 | tf_op jit(solution)/shard_map/ppermute | solution.py:116
  58.2 23.6 %collective-permute-start.11 = (bf16[2048,128]{1,0:T(8,128)(2,1)S(1)}, bf16[2048,128]{1,0:T(8,128)(2,1)S(1)}, u32[]{:S(2)}, u32[]{:S(2)}) collective-permute-start(bf16[2048,128]{1,0:T(8,128)(2,1)S(1)} %get-tuple-element.49), channel_id=1, source_target_pairs={{0,2},{2,4},{4,6},{6,0},{1,3},{3,5},{5,7},{7,1},{8,10},{10,12},{12... | collective-permute-start | bytes 1572872 | tf_op jit(solution)/shard_map/ppermute | solution.py:116
  62.7 21.6 %collective-permute-start.4 = (bf16[32,8192]{1,0:T(8,128)(2,1)S(1)}, bf16[32,8192]{1,0:T(8,128)(2,1)S(1)}, u32[]{:S(2)}, u32[]{:S(2)}) collective-permute-start(bf16[32,8192]{1,0:T(8,128)(2,1)S(1)} %get-tuple-element.43), channel_id=1, source_target_pairs={{0,56},{8,0},{16,8},{24,16},{32,24},{40,32},{48,40},{56,48},{1,57}... | collective-permute-start | bytes 1572872 | tf_op jit(solution)/shard_map/ppermute | solution.py:116
  67.0 19.9 %collective-permute-start.1 = (bf16[32,8192]{1,0:T(8,128)(2,1)S(1)}, bf16[32,8192]{1,0:T(8,128)(2,1)S(1)}, u32[]{:S(2)}, u32[]{:S(2)}) collective-permute-start(bf16[32,8192]{1,0:T(8,128)(2,1)S(1)} %add_convert_fusion.4), channel_id=1, source_target_pairs={{0,8},{8,16},{16,24},{24,32},{32,40},{40,48},{48,56},{56,0},{1,9},... | collective-permute-start | bytes 1572872 | tf_op jit(solution)/shard_map/ppermute | solution.py:116
  70.7 58.7 %collective-permute-start.10 = (bf16[2048,128]{1,0:T(8,128)(2,1)S(1)}, bf16[2048,128]{1,0:T(8,128)(2,1)S(1)}, u32[]{:S(2)}, u32[]{:S(2)}) collective-permute-start(bf16[2048,128]{1,0:T(8,128)(2,1)S(1)} %get-tuple-element.44), channel_id=1, source_target_pairs={{0,4},{2,6},{4,0},{6,2},{1,5},{3,7},{5,1},{7,3},{8,12},{10,14},{12... | collective-permute-start | bytes 1572872 | tf_op jit(solution)/shard_map/ppermute | solution.py:116
  79.0 50.4 %collective-permute-start.9 = (bf16[2048,128]{1,0:T(8,128)(2,1)S(1)}, bf16[2048,128]{1,0:T(8,128)(2,1)S(1)}, u32[]{:S(2)}, u32[]{:S(2)}) collective-permute-start(bf16[2048,128]{1,0:T(8,128)(2,1)S(1)} %get-tuple-element.45), channel_id=1, source_target_pairs={{0,6},{2,0},{4,2},{6,4},{1,7},{3,1},{5,3},{7,5},{8,14},{10,8},{12,... | collective-permute-start | bytes 1572872 | tf_op jit(solution)/shard_map/ppermute | solution.py:116
  81.8 47.7 %collective-permute-start.8 = (bf16[2048,128]{1,0:T(8,128)(2,1)S(1)}, bf16[2048,128]{1,0:T(8,128)(2,1)S(1)}, u32[]{:S(2)}, u32[]{:S(2)}) collective-permute-start(bf16[2048,128]{1,0:T(8,128)(2,1)S(1)} %get-tuple-element.46), channel_id=1, source_target_pairs={{0,2},{2,4},{4,6},{6,0},{1,3},{3,5},{5,7},{7,1},{8,10},{10,12},{12... | collective-permute-start | bytes 1572872 | tf_op jit(solution)/shard_map/ppermute | solution.py:116
  84.3 26.1 %collective-permute-start.13 = (bf16[2048,128]{1,0:T(8,128)(2,1)S(1)}, bf16[2048,128]{1,0:T(8,128)(2,1)S(1)}, u32[]{:S(2)}, u32[]{:S(2)}) collective-permute-start(bf16[2048,128]{1,0:T(8,128)(2,1)S(1)} %get-tuple-element.50), channel_id=1, source_target_pairs={{0,4},{2,6},{4,0},{6,2},{1,5},{3,7},{5,1},{7,3},{8,12},{10,14},{12... | collective-permute-start | bytes 1572872 | tf_op jit(solution)/shard_map/ppermute | solution.py:116
  86.9 37.5 %collective-permute-start.12 = (bf16[2048,128]{1,0:T(8,128)(2,1)S(1)}, bf16[2048,128]{1,0:T(8,128)(2,1)S(1)}, u32[]{:S(2)}, u32[]{:S(2)}) collective-permute-start(bf16[2048,128]{1,0:T(8,128)(2,1)S(1)} %get-tuple-element.51), channel_id=1, source_target_pairs={{0,6},{2,0},{4,2},{6,4},{1,7},{3,1},{5,3},{7,5},{8,14},{10,8},{12,... | collective-permute-start | bytes 1572872 | tf_op jit(solution)/shard_map/ppermute | solution.py:116
  110.4 34.2 %collective-permute-start.2 = (bf16[32,8192]{1,0:T(8,128)(2,1)S(1)}, bf16[32,8192]{1,0:T(8,128)(2,1)S(1)}, u32[]{:S(2)}, u32[]{:S(2)}) collective-permute-start(bf16[32,8192]{1,0:T(8,128)(2,1)S(1)} %get-tuple-element.40), channel_id=1, source_target_pairs={{0,8},{8,16},{16,24},{24,32},{32,40},{40,48},{48,56},{56,0},{1,9},... | collective-permute-start | bytes 1572872 | tf_op jit(solution)/shard_map/ppermute | solution.py:116
  124.3 20.3 %collective-permute-start.5 = (bf16[32,8192]{1,0:T(8,128)(2,1)S(1)}, bf16[32,8192]{1,0:T(8,128)(2,1)S(1)}, u32[]{:S(2)}, u32[]{:S(2)}) collective-permute-start(bf16[32,8192]{1,0:T(8,128)(2,1)S(1)} %get-tuple-element.41), channel_id=1, source_target_pairs={{0,56},{8,0},{16,8},{24,16},{32,24},{40,32},{48,40},{56,48},{1,57}... | collective-permute-start | bytes 1572872 | tf_op jit(solution)/shard_map/ppermute | solution.py:116
  129.4 32.2 %copy-start.4 = (bf16[1,1,2,16,8192]{4,3,2,1,0:T(8,128)(2,1)S(1)}, bf16[1,1,2,16,8192]{4,3,2,1,0:T(8,128)(2,1)}, u32[]{:S(2)}) copy-start(bf16[1,1,2,16,8192]{4,3,2,1,0:T(8,128)(2,1)} %param.9) | copy-start | bytes 1572868
  129.7 31.5 %collective-permute-start.14 = (bf16[1024,128]{1,0:T(8,128)(2,1)S(1)}, bf16[1024,128]{1,0:T(8,128)(2,1)S(1)}, u32[]{:S(2)}, u32[]{:S(2)}) collective-permute-start(bf16[1024,128]{1,0:T(8,128)(2,1)S(1)} %select_convert_fusion), channel_id=1, source_target_pairs={{0,1},{1,0},{2,3},{3,2},{4,5},{5,4},{6,7},{7,6},{8,9},{9,8},{10,11... | collective-permute-start | bytes 786440 | tf_op jit(solution)/shard_map/ppermute | solution.py:142
  144.9 17.7 %copy-start.7 = (bf16[1,1,16,8192]{3,2,1,0:T(8,128)(2,1)S(1)}, bf16[1,1,16,8192]{3,2,1,0:T(8,128)(2,1)}, u32[]{:S(2)}) copy-start(bf16[1,1,16,8192]{3,2,1,0:T(8,128)(2,1)} %param.14) | copy-start | bytes 786436
  144.9 16.7 %collective-permute-start.3 = (bf16[32,8192]{1,0:T(8,128)(2,1)S(1)}, bf16[32,8192]{1,0:T(8,128)(2,1)S(1)}, u32[]{:S(2)}, u32[]{:S(2)}) collective-permute-start(bf16[32,8192]{1,0:T(8,128)(2,1)S(1)} %get-tuple-element.38), channel_id=1, source_target_pairs={{0,8},{8,16},{16,24},{24,32},{32,40},{40,48},{48,56},{56,0},{1,9},... | collective-permute-start | bytes 1572872 | tf_op jit(solution)/shard_map/ppermute | solution.py:116
  147.0 14.6 %collective-permute-start.6 = (bf16[32,8192]{1,0:T(8,128)(2,1)S(1)}, bf16[32,8192]{1,0:T(8,128)(2,1)S(1)}, u32[]{:S(2)}, u32[]{:S(2)}) collective-permute-start(bf16[32,8192]{1,0:T(8,128)(2,1)S(1)} %get-tuple-element.39), channel_id=1, source_target_pairs={{0,56},{8,0},{16,8},{24,16},{32,24},{40,32},{48,40},{56,48},{1,57}... | collective-permute-start | bytes 1572872 | tf_op jit(solution)/shard_map/ppermute | solution.py:116
  151.7 33.3 %collective-permute-start.15 = (bf16[1024,128]{1,0:T(8,128)(2,1)S(1)}, bf16[1024,128]{1,0:T(8,128)(2,1)S(1)}, u32[]{:S(2)}, u32[]{:S(2)}) collective-permute-start(bf16[1024,128]{1,0:T(8,128)(2,1)S(1)} %select_convert_fusion.1), channel_id=1, source_target_pairs={{0,1},{1,0},{2,3},{3,2},{4,5},{5,4},{6,7},{7,6},{8,9},{9,8},{10,11... | collective-permute-start | bytes 786440 | tf_op jit(solution)/shard_map/ppermute | solution.py:142
  162.1 24.8 %copy-start.6 = (bf16[1,16,8192]{2,1,0:T(8,128)(2,1)S(1)}, bf16[1,16,8192]{2,1,0:T(8,128)(2,1)}, u32[]{:S(2)}) copy-start(bf16[1,16,8192]{2,1,0:T(8,128)(2,1)} %param.15) | copy-start | bytes 786436
  162.6 24.2 %collective-permute-start.7 = (bf16[16,8192]{1,0:T(8,128)(2,1)S(1)}, bf16[16,8192]{1,0:T(8,128)(2,1)S(1)}, u32[]{:S(2)}, u32[]{:S(2)}) collective-permute-start(bf16[16,8192]{1,0:T(8,128)(2,1)S(1)} %fusion.24), channel_id=1, source_target_pairs={{64,0},{128,64},{192,128},{256,192},{320,256},{384,320},{448,384},... | collective-permute-start | bytes 786440 | tf_op jit(solution)/shard_map/ppermute | solution.py:220
